TPU v7x, 32 devices: a whole 2x2x4 slice. The times are simulated.
32 devices in a mesh: lat: 16 (over z, y, x), batch: 2 (over core).
Axes of the slice: x: 2, y: 2, z: 4, core: 2. Of those that a mesh axis runs over, the one named last changes fastest.
Arguments:
- fields: bfloat16 [2, 192, 384, 384], P('batch', 'lat'), may hold values from -6 to 6
- cotangent: bfloat16 [2, 192, 384, 384], P('batch', 'lat'), may hold values from -6 to 6
- weights: bfloat16 [128, 2, 384, 384], P('lat'), may hold values from -0.21875 to 0.21875
- degree_of: int32 [128], replicated, may hold values from 0 to 127, each once
Outputs:
- grad_fields: bfloat16 [2, 192, 384, 384], P('batch', 'lat')
- grad_weights: bfloat16 [128, 2, 384, 384], P('lat')
Inputs may be any that keep to these rules, and one draw needn't show every extreme that they name: `degree_of`: each degree 0 to 127 is held by exactly one slot.
All inputs are finite; a program needn't handle non-finite values.
Results may differ from a plain program's by a relative error of at most 0.018.
Values may be sent and summed in bfloat16 or wider, within the bound.
A program may use at most 64 MiB of HBM per device.

v0:
```python
import functools

import jax
import numpy as np
import jax.numpy as jnp
from jax import lax
from jax.experimental import pallas as pl
from jax.experimental.pallas import tpu as pltpu
from jax.sharding import PartitionSpec as P

LATS = 192
LONS = 384
ORDERS = 128
DEGREES = 128
CHANNELS = 384
LANES = 128


def table_kernel(deg_ref, diag_ref, cos_ref, quad_ref, order_ref, q_ref, p_ref, slot_ref, rows_ref):
    orders = diag_ref.shape[0]
    lats = q_ref.shape[2]
    degrees = deg_ref.shape[0]

    def invert(slot, carry):
        slot_ref[deg_ref[slot]] = slot
        return carry

    lax.fori_loop(0, degrees, invert, 0)
    order_real = order_ref[...]
    squared = order_real * order_real
    diagonal = diag_ref[...]
    cosine = cos_ref[...]
    first_lead = jnp.sqrt(2.0 * order_real + 3.0)
    halves = rows_ref.shape[0]

    def advance(degree, carry):
        previous, older = carry
        degree_real = degree.astype(jnp.float32)
        lead = jnp.sqrt(
            jnp.maximum(4.0 * degree_real * degree_real - 1.0, 0.0)
            / jnp.maximum(degree_real * degree_real - squared, 1.0)
        )
        lower = degree_real - 1.0
        back = jnp.sqrt(
            jnp.maximum(lower * lower - squared, 0.0) / jnp.maximum(4.0 * lower * lower - 1.0, 1.0)
        )
        general = lead * (cosine * previous - back * older)
        first = first_lead * cosine * previous
        value = jnp.where(
            degree_real == order_real,
            diagonal,
            jnp.where(
                degree_real == order_real + 1.0,
                first,
                jnp.where(degree_real > order_real + 1.0, general, 0.0),
            ),
        )
        slot = slot_ref[degree]
        for half in range(halves):
            rows_ref[half, pl.ds(slot, orders, stride=degrees), :] = value[
                :, half * LANES : (half + 1) * LANES
            ]
        return (value, previous)

    zeros = diagonal * 0.0
    lax.fori_loop(0, degrees, advance, (zeros, zeros), unroll=4)
    quadrature = quad_ref[...]
    for order in range(orders):
        for half in range(halves):
            low = half * LANES
            high = min(lats, low + LANES)
            chosen = rows_ref[half, order * degrees : (order + 1) * degrees, :][:, : high - low]
            p_ref[order, :, low:high] = chosen.astype(jnp.bfloat16)
            q_ref[order, :, low:high] = (chosen * quadrature[:, low:high]).astype(jnp.bfloat16)


def spectral_tables(start, ord_dev, degree_of):
    halves = -(-LATS // LANES)
    padded = halves * LANES
    order_col = (start + jnp.arange(ord_dev, dtype=jnp.int32)).astype(jnp.float32)[:, None]
    lat_ids = jnp.minimum(jnp.arange(padded, dtype=jnp.float32), LATS - 1.0)
    colatitude = jnp.pi * (lat_ids + 0.5) / LATS
    sine = jnp.sin(colatitude)[None, :]
    steps_up = jnp.arange(1, DEGREES + 1, dtype=jnp.float32)[None, :]
    factor = jnp.where(
        steps_up <= order_col, 0.5 * jnp.log((2.0 * steps_up + 1.0) / (2.0 * steps_up)), 0.0
    )
    log_start = 0.5 * jnp.log(1.0 / (4.0 * jnp.pi)) + jnp.sum(factor, axis=1, keepdims=True)
    diagonal = jnp.exp(log_start + order_col * jnp.log(sine))
    cosine = jnp.broadcast_to(jnp.cos(colatitude)[None, :], diagonal.shape)
    quadrature = 2.0 * jnp.pi * jnp.pi / LATS * sine
    orders = jnp.broadcast_to(order_col, diagonal.shape)
    vmem = pl.BlockSpec(memory_space=pltpu.VMEM)
    shape = jax.ShapeDtypeStruct((ord_dev, DEGREES, LATS), jnp.bfloat16)
    return pl.pallas_call(
        table_kernel,
        out_shape=(shape, shape),
        in_specs=[pl.BlockSpec(memory_space=pltpu.SMEM)] + [vmem] * 4,
        out_specs=(vmem, vmem),
        scratch_shapes=[
            pltpu.SMEM((DEGREES,), jnp.int32),
            pltpu.VMEM((halves, ord_dev * DEGREES, LANES), jnp.float32),
        ],
        name="legendre_tables",
    )(degree_of, diagonal, cosine, quadrature, orders)


def fourier_tables(lon_count, order_count):
    lon_ids = jnp.arange(lon_count, dtype=jnp.int32)[:, None]
    order_ids = jnp.arange(order_count, dtype=jnp.int32)[None, :]
    phase = 2.0 * jnp.pi * (lon_ids * order_ids % lon_count).astype(jnp.float32) / lon_count
    forward = (
        jnp.stack([jnp.cos(phase), -jnp.sin(phase)], axis=2).reshape(lon_count, 2 * order_count)
        / lon_count
    )
    doubled = jnp.where(order_ids == 0, 1.0, 2.0)
    inverse = jnp.stack([doubled * jnp.cos(phase), -doubled * jnp.sin(phase)], axis=2).reshape(
        lon_count, 2 * order_count
    )
    return (forward.astype(jnp.bfloat16), jnp.transpose(inverse).astype(jnp.bfloat16))


def to_orders(values):
    return lax.all_to_all(values, "lat", split_axis=1, concat_axis=0, tiled=True)


def to_degrees(values):
    return lax.all_to_all(values, "lat", split_axis=0, concat_axis=1, tiled=True)


def back_to_orders(values):
    return lax.all_to_all(values, "lat", split_axis=1, concat_axis=0, tiled=True)


def to_bands(values):
    return lax.all_to_all(values, "lat", split_axis=0, concat_axis=1, tiled=True)


def product(spec, left, right):
    return jnp.einsum(spec, left, right, preferred_element_type=jnp.float32)


def apply_filter(coeffs, weights):
    c_real = coeffs[:, :, 0]
    c_imag = coeffs[:, :, 1]
    w_real = weights[:, 0]
    w_imag = weights[:, 1]
    f_real = product("jmsc,jcd->jmsd", c_real, w_real) - product("jmsc,jcd->jmsd", c_imag, w_imag)
    f_imag = product("jmsc,jcd->jmsd", c_real, w_imag) + product("jmsc,jcd->jmsd", c_imag, w_real)
    return jnp.stack([f_real, f_imag], axis=2).astype(jnp.bfloat16)


def adjoint_filter(grads, weights):
    g_real = grads[:, :, 0]
    g_imag = grads[:, :, 1]
    w_real = weights[:, 0]
    w_imag = weights[:, 1]
    a_real = product("jmsd,jcd->jmsc", g_real, w_real) + product("jmsd,jcd->jmsc", g_imag, w_imag)
    a_imag = product("jmsd,jcd->jmsc", g_imag, w_real) - product("jmsd,jcd->jmsc", g_real, w_imag)
    return jnp.stack([a_real, a_imag], axis=2).astype(jnp.bfloat16)


def filter_grad(coeffs, grads):
    c_real = coeffs[:, :, 0]
    c_imag = coeffs[:, :, 1]
    g_real = grads[:, :, 0]
    g_imag = grads[:, :, 1]
    dw_real = product("jmsc,jmsd->jcd", c_real, g_real) + product("jmsc,jmsd->jcd", c_imag, g_imag)
    dw_imag = product("jmsc,jmsd->jcd", c_real, g_imag) - product("jmsc,jmsd->jcd", c_imag, g_real)
    return jnp.stack([dw_real, dw_imag], axis=1)


def constant_tables(orders):
    padded = -(-LATS // LANES) * LANES
    lat_ids = np.minimum(np.arange(padded), LATS - 1)
    colatitude = np.pi * (lat_ids + 0.5) / LATS
    sine = np.sin(colatitude)[None, :]
    ids = np.arange(ORDERS)
    steps_up = np.arange(1, ORDERS + 1)
    growth = np.cumsum(0.5 * np.log((2.0 * steps_up + 1.0) / (2.0 * steps_up)))
    log_start = 0.5 * np.log(1.0 / (4.0 * np.pi)) + np.concatenate([[0.0], growth[:-1]])
    diagonal = np.exp(log_start[:, None] + ids[:, None] * np.log(sine))
    cosine = np.broadcast_to(np.cos(colatitude)[None, :], (orders, padded))
    quadrature = 2.0 * np.pi * np.pi / LATS * sine
    phase = 2.0 * np.pi * (np.arange(LONS)[:, None] * ids[None, :] % LONS) / LONS
    forward = np.stack([np.cos(phase), -np.sin(phase)], axis=2).reshape(LONS, -1) / LONS
    doubled = np.where(ids == 0, 1.0, 2.0)[None, :]
    inverse = np.stack([doubled * np.cos(phase), -doubled * np.sin(phase)], axis=2)
    inverse = inverse.reshape(LONS, -1)
    floats = [jnp.asarray(t, jnp.float32) for t in (diagonal, cosine, quadrature)]
    waves = [forward.T, forward, inverse.T, inverse]
    halves = [jnp.asarray(np.float32(t).astype(jnp.bfloat16)) for t in waves]
    return floats, halves


def fill_tables(first_order, deg_ref, diag_ref, cos_ref, quad_ref, qtab, ptab, table, by_slot):
    orders, degrees, lats = qtab.shape
    halves = by_slot.shape[0]
    diagonal = diag_ref[pl.ds(pl.multiple_of(first_order, orders), orders), :]
    cosine = cos_ref[...]
    order_ids = first_order + lax.broadcasted_iota(jnp.int32, diagonal.shape, 0)
    order_real = order_ids.astype(jnp.float32)
    squared = order_real * order_real
    first_lead = jnp.sqrt(2.0 * order_real + 3.0)

    def advance(degree, carry):
        previous, older = carry
        degree_real = degree.astype(jnp.float32)
        lead = jnp.sqrt(
            jnp.maximum(4.0 * degree_real * degree_real - 1.0, 0.0)
            / jnp.maximum(degree_real * degree_real - squared, 1.0)
        )
        lower = degree_real - 1.0
        back = jnp.sqrt(
            jnp.maximum(lower * lower - squared, 0.0) / jnp.maximum(4.0 * lower * lower - 1.0, 1.0)
        )
        general = lead * (cosine * previous - back * older)
        first = first_lead * cosine * previous
        value = jnp.where(
            order_ids == degree,
            diagonal,
            jnp.where(
                order_ids + 1 == degree, first, jnp.where(order_ids + 1 < degree, general, 0.0)
            ),
        )
        table[degree] = value
        return (value, previous)

    zeros = diagonal * 0.0
    lax.fori_loop(0, degrees, advance, (zeros, zeros), unroll=2)

    def place(slot, carry):
        value = table[deg_ref[slot]]
        for half in range(halves):
            by_slot[half, pl.ds(slot, orders, stride=degrees), :] = value[
                :, half * LANES : (half + 1) * LANES
            ]
        return carry

    lax.fori_loop(0, degrees, place, 0)
    quadrature = quad_ref[...]
    for order in range(orders):
        for half in range(halves):
            low = half * LANES
            high = min(lats, low + LANES)
            chosen = by_slot[half, order * degrees : (order + 1) * degrees, :][:, : high - low]
            ptab[order, :, low:high] = chosen.astype(jnp.bfloat16)
            qtab[order, :, low:high] = (chosen * quadrature[:, low:high]).astype(jnp.bfloat16)


def pair_swap(values, even_sign):
    rows = values.shape[0]
    even = lax.broadcasted_iota(jnp.int32, values.shape, 0) % 2 == 0
    above = pltpu.roll(values, rows - 1, 0)
    below = pltpu.roll(values, 1, 0)
    return jnp.where(even, even_sign * above, -even_sign * below)


def gelu_slope(x):
    scale = 0.7978845608028654
    square = x * x
    t = jnp.tanh(scale * (x + 0.044715 * x * square))
    return 0.5 * (1.0 + t) + 0.5 * x * (1.0 - t * t) * (scale * (1.0 + 0.134145 * square))


def dot(left, right, dims=((1,), (0,))):
    return lax.dot_general(left, right, (dims, ((), ())), preferred_element_type=jnp.float32)


def block_kernel(
    n, nb, fields, cotangent, weights, deg_ref, diag_ref, cos_ref, quad_ref,
    fwd_fk, fwd_kf, inv_fk, inv_kf,
    grad_out, dw_out,
    fbuf, cbuf, wbuf, band_out, band_in, ord_in, ord_out, deg_out, deg_back, co, go, mixed,
    wide_a, wide_b, dw, dw_in, qtab, ptab, table, by_slot,
    load_sem, send_sem, recv_sem, dw_send, dw_recv, out_sem,
):
    me = lax.axis_index("lat")
    me_b = lax.axis_index("batch")
    chunks, lat_dev = fbuf.shape[0], fbuf.shape[1]
    orders = qtab.shape[0]
    rows = 2 * orders
    slots = co.shape[1]
    degrees = n * slots
    lats = n * lat_dev
    mesh_id = pl.DeviceIdType.MESH

    def lanes(chunk):
        return pl.ds(chunk * LANES, LANES)

    def load(chunk):
        return pltpu.make_async_copy(
            fields.at[0, :, :, lanes(chunk)], fbuf.at[chunk], load_sem.at[chunk]
        )

    def load_cot(chunk):
        return pltpu.make_async_copy(
            cotangent.at[0, :, :, lanes(chunk)], cbuf.at[chunk], load_sem.at[chunks + chunk]
        )

    load_w = pltpu.make_async_copy(weights, wbuf, load_sem.at[2 * chunks])
    for chunk in range(chunks):
        load(chunk).start()
    load_w.start()
    for chunk in range(chunks):
        load_cot(chunk).start()

    barrier = pltpu.get_barrier_semaphore()

    def greet(step, carry):
        peer = lax.rem(me + step, n)
        pl.semaphore_signal(barrier, inc=1, device_id={"lat": peer}, device_id_type=mesh_id)
        return carry

    lax.fori_loop(1, n, greet, 0)
    for step in range(1, nb):
        peer = lax.rem(me_b + step, nb)
        pl.semaphore_signal(barrier, inc=1, device_id={"batch": peer}, device_id_type=mesh_id)
    pl.semaphore_wait(barrier, n - 1 + nb - 1)

    def part(ref, chunk, kind, owner):
        if kind == "band":
            return ref.at[chunk, :, pl.ds(pl.multiple_of(owner * rows, rows), rows), :]
        if kind == "lat":
            return ref.at[chunk, pl.ds(owner * lat_dev, lat_dev)]
        return ref.at[chunk, pl.ds(owner * slots, slots)]

    def exchange(stage, chunk, source, source_kind, target, target_kind):
        def send(step, carry):
            peer = lax.rem(me + 1 + lax.rem((step - 1) * max(n // 4, 1), n - 1), n)
            pltpu.make_async_remote_copy(
                src_ref=part(source, chunk, source_kind, peer),
                dst_ref=part(target, chunk, target_kind, me),
                send_sem=send_sem.at[stage, chunk],
                recv_sem=recv_sem.at[stage, chunk],
                device_id={"lat": peer},
                device_id_type=mesh_id,
            ).start()
            return carry

        lax.fori_loop(1, n, send, 0)
        pltpu.make_async_copy(
            part(source, chunk, source_kind, me),
            part(target, chunk, target_kind, me),
            recv_sem.at[stage, chunk],
        ).start()

    def arrived(stage, chunk, target):
        pltpu.make_async_copy(target.at[chunk], target.at[chunk], recv_sem.at[stage, chunk]).wait()

    def departed(stage, chunk, source, kind):
        if kind == "band":
            view = source.at[chunk, :, 0 : (n - 1) * rows, :]
        elif kind == "lat":
            view = source.at[chunk, 0 : (n - 1) * lat_dev]
        else:
            view = source.at[chunk, 0 : (n - 1) * slots]
        pltpu.make_async_copy(view, view, send_sem.at[stage, chunk]).wait()

    def widen(source, chunk, depth):
        def one(block, carry):
            piece = source[chunk, pl.ds(block * depth, depth)].astype(jnp.float32)
            wide_a[pl.ds(pl.multiple_of(block * depth * rows, depth * rows), depth * rows), :] = (
                piece.reshape(depth * rows, LANES)
            )
            return carry

        lax.fori_loop(0, n, one, 0)

    def narrow(target, chunk, depth):
        def one(block, carry):
            start = pl.multiple_of(block * depth * rows, depth * rows)
            piece = wide_b[pl.ds(start, depth * rows), :]
            target[chunk, pl.ds(block * depth, depth)] = piece.reshape(
                depth, rows, LANES
            ).astype(jnp.bfloat16)
            return carry

        lax.fori_loop(0, n, one, 0)

    def apply_table(table, depth_in, depth_out, dims):
        def one(order, carry):
            real = wide_a[pl.ds(2 * order, depth_in, stride=rows), :]
            imag = wide_a[pl.ds(2 * order + 1, depth_in, stride=rows), :]
            both = jnp.concatenate([real, imag], axis=1).astype(jnp.bfloat16)
            result = dot(table[order], both, dims)
            wide_b[pl.ds(2 * order, depth_out, stride=rows), :] = result[:, :LANES]
            wide_b[pl.ds(2 * order + 1, depth_out, stride=rows), :] = result[:, LANES:]
            return carry

        lax.fori_loop(0, orders, one, 0)

    def analyse(stage, chunk, table, target, before):
        arrived(stage, chunk, ord_in)
        widen(ord_in, chunk, lat_dev)
        apply_table(table, lats, degrees, ((1,), (0,)))
        if before is not None:
            departed(before, chunk, deg_out, "slot")
        narrow(deg_out, chunk, slots)
        exchange(stage + 1, chunk, deg_out, "slot", target, "band")

    def synthesise(stage, chunk, table, before):
        arrived(stage, chunk, deg_back)
        widen(deg_back, chunk, slots)
        apply_table(table, degrees, lats, ((0,), (0,)))
        if before is not None:
            departed(before, chunk, ord_out, "lat")
        narrow(ord_out, chunk, lat_dev)
        exchange(stage + 1, chunk, ord_out, "lat", band_in, "band")

    def pair(source, chunk, row):
        return jnp.concatenate([source[chunk, 2 * row], source[chunk, 2 * row + 1]], axis=1)

    def put_pair(target, chunk, row, values):
        values = values.astype(jnp.bfloat16)
        target[chunk, 2 * row] = values[:, :LANES]
        target[chunk, 2 * row + 1] = values[:, LANES:]

    def joined(source, slot):
        return jnp.concatenate([source[chunk, slot] for chunk in range(chunks)], axis=1)

    for chunk in range(chunks):
        load(chunk).wait()

        def fourier(row, carry):
            put_pair(band_out, chunk, row, dot(fwd_fk[...], pair(fbuf, chunk, row)))
            return carry

        lax.fori_loop(0, lat_dev // 2, fourier, 0)
        exchange(0, chunk, band_out, "band", ord_in, "lat")
    fill_tables(
        me * orders, deg_ref, diag_ref, cos_ref, quad_ref, qtab, ptab, table, by_slot
    )
    for chunk in range(chunks):
        analyse(0, chunk, qtab, co, None)
    load_w.wait()
    for chunk in range(chunks):
        arrived(1, chunk, co)
    for chunk in range(chunks):

        def mix(slot, carry):
            values = joined(co, slot)
            span = slice(chunk * LANES, (chunk + 1) * LANES)
            both = dot(
                values, jnp.concatenate([wbuf[slot, 0, :, span], wbuf[slot, 1, :, span]], axis=1)
            )
            crossed = pair_swap(both[:, LANES:], -1.0)
            mixed[chunk, slot] = (both[:, :LANES] + crossed).astype(jnp.bfloat16)
            return carry

        lax.fori_loop(0, slots, mix, 0)
        exchange(2, chunk, mixed, "band", deg_back, "slot")
    for chunk in range(chunks):
        synthesise(2, chunk, ptab, None)
    for chunk in range(chunks):
        load_cot(chunk).wait()
        arrived(3, chunk, band_in)
        departed(0, chunk, band_out, "band")

        def middle(row, carry):
            response = dot(inv_kf[...], pair(band_in, chunk, row))
            upstream = pair(cbuf, chunk, row).astype(jnp.float32) * gelu_slope(response)
            put_pair(band_out, chunk, row, dot(inv_fk[...], upstream.astype(jnp.bfloat16)))
            return carry

        lax.fori_loop(0, lat_dev // 2, middle, 0)
        exchange(4, chunk, band_out, "band", ord_in, "lat")
    for chunk in range(chunks):
        analyse(4, chunk, ptab, go, 1)
    for chunk in range(chunks):
        arrived(5, chunk, go)
    for chunk in range(chunks):
        departed(2, chunk, mixed, "band")

        def adjoint(slot, carry):
            values = joined(go, slot)
            span = slice(chunk * LANES, (chunk + 1) * LANES)
            both = dot(
                values,
                jnp.concatenate([wbuf[slot, 0, span, :], wbuf[slot, 1, span, :]], axis=0),
                ((1,), (1,)),
            )
            crossed = pair_swap(both[:, LANES:], 1.0)
            mixed[chunk, slot] = (both[:, :LANES] + crossed).astype(jnp.bfloat16)
            return carry

        lax.fori_loop(0, slots, adjoint, 0)
        exchange(6, chunk, mixed, "band", deg_back, "slot")

    def weight_grad(slot, carry):
        values = joined(co, slot)
        grads = joined(go, slot)
        turned = pair_swap(grads.astype(jnp.float32), 1.0).astype(jnp.bfloat16)
        span = ((0,), (0,))
        dw[slot, 0] = dot(values, grads, span).astype(jnp.bfloat16)
        dw[slot, 1] = dot(values, turned, span).astype(jnp.bfloat16)
        return carry

    lax.fori_loop(0, slots, weight_grad, 0)
    dw_copies = []
    for step in range(1, nb):
        peer = lax.rem(me_b + step, nb)
        copy = pltpu.make_async_remote_copy(
            src_ref=dw,
            dst_ref=dw_in.at[step - 1],
            send_sem=dw_send.at[step - 1],
            recv_sem=dw_recv.at[step - 1],
            device_id={"batch": peer},
            device_id_type=mesh_id,
        )
        copy.start()
        dw_copies.append(copy)
    for chunk in range(chunks):
        synthesise(6, chunk, qtab, 3)
    for copy in dw_copies:
        copy.wait()

    def total(slot, carry):
        value = dw[slot].astype(jnp.float32)
        for step in range(nb - 1):
            value = value + dw_in[step, slot].astype(jnp.float32)
        dw[slot] = value.astype(jnp.bfloat16)
        return carry

    lax.fori_loop(0, slots, total, 0)
    store_w = pltpu.make_async_copy(dw, dw_out, out_sem.at[chunks])
    store_w.start()

    def store(chunk):
        return pltpu.make_async_copy(
            cbuf.at[chunk], grad_out.at[0, :, :, lanes(chunk)], out_sem.at[chunk]
        )

    for chunk in range(chunks):
        arrived(7, chunk, band_in)

        def finish(row, carry):
            delta = dot(fwd_kf[...], pair(band_in, chunk, row))
            put_pair(cbuf, chunk, row, pair(cbuf, chunk, row).astype(jnp.float32) + delta)
            return carry

        lax.fori_loop(0, lat_dev // 2, finish, 0)
        store(chunk).start()
    for chunk in range(chunks):
        departed(4, chunk, band_out, "band")
        departed(5, chunk, deg_out, "slot")
        departed(6, chunk, mixed, "band")
        departed(7, chunk, ord_out, "lat")
        store(chunk).wait()
    store_w.wait()


def local_kernel(fields, cotangent, weights, degree_of):
    if fields.shape[0] != 1 or fields.shape[1] % 2:
        return local(fields, cotangent, weights, degree_of)
    n = lax.axis_size("lat")
    nb = lax.axis_size("batch")
    lat_dev, lons, channels = fields.shape[1:]
    slots = weights.shape[0]
    orders = ORDERS // n
    rows = 2 * orders
    chunks = channels // LANES
    floats, waves = constant_tables(orders)
    halves = -(-LATS // LANES)
    vmem = pl.BlockSpec(memory_space=pltpu.VMEM)
    anywhere = pl.BlockSpec(memory_space=pl.ANY)

    def buffer(*dims):
        return pltpu.VMEM(dims, jnp.bfloat16)

    dma = pltpu.SemaphoreType.DMA
    others = max(nb - 1, 1)
    wide_rows = max(LATS, DEGREES) * rows
    return pl.pallas_call(
        functools.partial(block_kernel, n, nb),
        out_shape=(
            jax.ShapeDtypeStruct(fields.shape, jnp.bfloat16),
            jax.ShapeDtypeStruct(weights.shape, jnp.bfloat16),
        ),
        in_specs=[anywhere] * 3 + [pl.BlockSpec(memory_space=pltpu.SMEM)] + [vmem] * 7,
        out_specs=(anywhere, anywhere),
        scratch_shapes=[
            buffer(chunks, lat_dev, lons, LANES),
            buffer(chunks, lat_dev, lons, LANES),
            buffer(*weights.shape),
            buffer(chunks, lat_dev, n * rows, LANES),
            buffer(chunks, lat_dev, n * rows, LANES),
            buffer(chunks, LATS, rows, LANES),
            buffer(chunks, LATS, rows, LANES),
            buffer(chunks, DEGREES, rows, LANES),
            buffer(chunks, DEGREES, rows, LANES),
            buffer(chunks, slots, n * rows, LANES),
            buffer(chunks, slots, n * rows, LANES),
            buffer(chunks, slots, n * rows, LANES),
            pltpu.VMEM((wide_rows, LANES), jnp.float32),
            pltpu.VMEM((wide_rows, LANES), jnp.float32),
            buffer(*weights.shape),
            buffer(others, *weights.shape),
            buffer(orders, DEGREES, LATS),
            buffer(orders, DEGREES, LATS),
            pltpu.VMEM((DEGREES, orders, halves * LANES), jnp.float32),
            pltpu.VMEM((halves, orders * DEGREES, LANES), jnp.float32),
            dma((2 * chunks + 1,)),
            dma((8, chunks)),
            dma((8, chunks)),
            dma((others,)),
            dma((others,)),
            dma((chunks + 1,)),
        ],
        compiler_params=pltpu.CompilerParams(
            collective_id=0, has_side_effects=True, vmem_limit_bytes=60 * 2**20
        ),
        name="filter_block",
    )(
        fields, cotangent, weights, degree_of, *floats, *waves,
    )


def local(fields, cotangent, weights, degree_of):
    samples = fields.shape[0]
    band_rows = fields.shape[1]
    ord_dev = ORDERS // lax.axis_size("lat")
    forward, inverse = fourier_tables(LONS, ORDERS)
    qslot, pslot = spectral_tables(lax.axis_index("lat") * ord_dev, ord_dev, degree_of)
    spectra = product("sikc,kf->ifsc", fields, forward).astype(jnp.bfloat16)
    spectra = spectra.reshape(band_rows, ORDERS, 2, samples, CHANNELS)
    gathered = to_orders(spectra)
    coeffs_local = product("mji,imrsc->jmrsc", qslot, gathered).astype(jnp.bfloat16)
    coeffs = to_degrees(coeffs_local)
    filtered = apply_filter(coeffs, weights)
    returned = back_to_orders(filtered)
    synth_local = product("mji,jmrsc->imrsc", pslot, returned).astype(jnp.bfloat16)
    synth = to_bands(synth_local)
    response = product(
        "ifsc,fk->sikc", synth.reshape(band_rows, 2 * ORDERS, samples, CHANNELS), inverse
    )
    activated, pullback = jax.vjp(jax.nn.gelu, response)
    upstream = pullback(cotangent.astype(jnp.float32))[0].astype(jnp.bfloat16)
    grad_synth = product("sikc,fk->ifsc", upstream, inverse).astype(jnp.bfloat16)
    grad_synth = grad_synth.reshape(band_rows, ORDERS, 2, samples, CHANNELS)
    grad_gathered = to_orders(grad_synth)
    grad_local = product("mji,imrsc->jmrsc", pslot, grad_gathered).astype(jnp.bfloat16)
    grad_filtered = to_degrees(grad_local)
    weight_total = lax.psum(filter_grad(coeffs, grad_filtered).astype(jnp.bfloat16), "batch")
    grad_coeffs = adjoint_filter(grad_filtered, weights)
    grad_back = back_to_orders(grad_coeffs)
    grad_local_spec = product("mji,jmrsc->imrsc", qslot, grad_back).astype(jnp.bfloat16)
    grad_bands = to_bands(grad_local_spec)
    delta = product(
        "ifsc,kf->sikc", grad_bands.reshape(band_rows, 2 * ORDERS, samples, CHANNELS), forward
    )
    grad_fields = (cotangent.astype(jnp.float32) + delta).astype(jnp.bfloat16)
    return (grad_fields, weight_total)


def solution(mesh):
    orders = ORDERS // mesh.shape["lat"]
    return jax.shard_map(
        local_kernel if orders % 8 == 0 and CHANNELS % LANES == 0 else local,
        mesh=mesh,
        in_specs=(
            P("batch", "lat", None, None),
            P("batch", "lat", None, None),
            P("lat", None, None, None),
            P(),
        ),
        out_specs=(P("batch", "lat", None, None), P("lat", None, None, None)),
        check_vma=False,
    )
```

profile of v0, /device:TPU:0, one launch (start us, length us, event | category | flops | bytes accessed | tf_op | source)
XLA Modules:
  0.0 363.9 jit_solution(17076271984684913571)
XLA Ops:
  0.6 356.7 %filter_block.1 = (bf16[1,12,384,384]{3,2,1,0:T(8,128)(2,1)}, bf16[8,2,384,384]{3,2,1,0:T(8,128)(2,1)}) custom-call(bf16[1,12,384,384]{3,2,1,0:T(8,128)(2,1)} %fields.1, bf16[1,12,384,384]{3,2,1,0:T(8,128)(2,1)} %cotangent.1, bf16[8,2,384,384]{3,2,1,0:T(8,128)(2,1)} %weights.1, s32[128]{0:T(128)} %deg_ref.1, f32[128,256]{1,0:T(8,128)} %constant.14.clone.diag_ref, ...), custom_call_target="tpu_custom_call" | custom-call | tf_op jit(solution)/shard_map/filter_block/pallas_call | solution.py:574
  357.4 0.0 copy-start
  357.4 4.3 %copy.15 = bf16[1,12,384,384]{3,2,1,0:T(8,128)(2,1)} copy(bf16[1,12,384,384]{3,2,1,0:T(8,128)(2,1)} %get-tuple-element.4) | data formatting | bytes 7077888
  361.7 0.0 copy-done
  361.7 2.2 copy.16
Async XLA Ops:
  357.4 4.3 %copy-start = (bf16[8,2,384,384]{3,2,1,0:T(8,128)(2,1)S(1)}, bf16[8,2,384,384]{3,2,1,0:T(8,128)(2,1)}, u32[]{:S(2)}) copy-start(bf16[8,2,384,384]{3,2,1,0:T(8,128)(2,1)} %get-tuple-element.5) | copy-start | bytes 14155780
where the time goes:
time: 364 us
  Pallas kernels  357 us (98%)
  local copies, waits for them, and re-layouts  6.5 us (2%)
    pallas_call x1, Pallas kernels, local_kernel(): pl.pallas_call(functools.partial(block_kernel, n, nb), out_shape=(jax.Sha...  357 us

commit v1 on v0

--- a/solution.py
+++ b/solution.py
@@ -14,6 +14,7 @@
 DEGREES = 128
 CHANNELS = 384
 LANES = 128
+GROUP = 8
 
 
 def table_kernel(deg_ref, diag_ref, cos_ref, quad_ref, order_ref, q_ref, p_ref, slot_ref, rows_ref):
@@ -170,18 +171,19 @@
     return jnp.stack([dw_real, dw_imag], axis=1)
 
 
-def constant_tables(orders):
-    padded = -(-LATS // LANES) * LANES
-    lat_ids = np.minimum(np.arange(padded), LATS - 1)
+def constant_tables():
+    sides = 2
+    half = LATS // sides
+    lat_ids = np.minimum(np.arange(LANES)[None, :], half - 1) + half * np.arange(sides)[:, None]
     colatitude = np.pi * (lat_ids + 0.5) / LATS
-    sine = np.sin(colatitude)[None, :]
+    sine = np.sin(colatitude)[:, None, :]
     ids = np.arange(ORDERS)
     steps_up = np.arange(1, ORDERS + 1)
     growth = np.cumsum(0.5 * np.log((2.0 * steps_up + 1.0) / (2.0 * steps_up)))
     log_start = 0.5 * np.log(1.0 / (4.0 * np.pi)) + np.concatenate([[0.0], growth[:-1]])
-    diagonal = np.exp(log_start[:, None] + ids[:, None] * np.log(sine))
-    cosine = np.broadcast_to(np.cos(colatitude)[None, :], (orders, padded))
-    quadrature = 2.0 * np.pi * np.pi / LATS * sine
+    diagonal = np.exp(log_start[None, :, None] + ids[None, :, None] * np.log(sine))
+    cosine = np.broadcast_to(np.cos(colatitude)[:, None, :], (sides, GROUP, LANES))
+    quadrature = np.broadcast_to(2.0 * np.pi * np.pi / LATS * sine, (sides, GROUP, LANES))
     phase = 2.0 * np.pi * (np.arange(LONS)[:, None] * ids[None, :] % LONS) / LONS
     forward = np.stack([np.cos(phase), -np.sin(phase)], axis=2).reshape(LONS, -1) / LONS
     doubled = np.where(ids == 0, 1.0, 2.0)[None, :]
@@ -193,59 +195,66 @@
     return floats, halves
 
 
-def fill_tables(first_order, deg_ref, diag_ref, cos_ref, quad_ref, qtab, ptab, table, by_slot):
-    orders, degrees, lats = qtab.shape
-    halves = by_slot.shape[0]
-    diagonal = diag_ref[pl.ds(pl.multiple_of(first_order, orders), orders), :]
-    cosine = cos_ref[...]
-    order_ids = first_order + lax.broadcasted_iota(jnp.int32, diagonal.shape, 0)
-    order_real = order_ids.astype(jnp.float32)
-    squared = order_real * order_real
-    first_lead = jnp.sqrt(2.0 * order_real + 3.0)
+def fill_tables(side, firsts, deg_ref, diag_ref, cos_ref, quad_ref, qtab, ptab, table, by_slot):
+    kinds, orders, degrees, lats = qtab.shape
+    every = kinds * orders
+    cosine = cos_ref[side]
+    diagonal, ids, squared, first_lead = [], [], [], []
+    for first in firsts:
+        diagonal.append(diag_ref[side, pl.ds(pl.multiple_of(first, orders), orders), :])
+        ids.append(first + lax.broadcasted_iota(jnp.int32, cosine.shape, 0))
+        real = ids[-1].astype(jnp.float32)
+        squared.append(real * real)
+        first_lead.append(jnp.sqrt(2.0 * real + 3.0))
 
     def advance(degree, carry):
-        previous, older = carry
         degree_real = degree.astype(jnp.float32)
-        lead = jnp.sqrt(
-            jnp.maximum(4.0 * degree_real * degree_real - 1.0, 0.0)
-            / jnp.maximum(degree_real * degree_real - squared, 1.0)
-        )
         lower = degree_real - 1.0
-        back = jnp.sqrt(
-            jnp.maximum(lower * lower - squared, 0.0) / jnp.maximum(4.0 * lower * lower - 1.0, 1.0)
-        )
-        general = lead * (cosine * previous - back * older)
-        first = first_lead * cosine * previous
-        value = jnp.where(
-            order_ids == degree,
-            diagonal,
-            jnp.where(
-                order_ids + 1 == degree, first, jnp.where(order_ids + 1 < degree, general, 0.0)
-            ),
-        )
-        table[degree] = value
-        return (value, previous)
-
-    zeros = diagonal * 0.0
-    lax.fori_loop(0, degrees, advance, (zeros, zeros), unroll=2)
+        state = []
+        for kind in range(kinds):
+            previous, older = carry[kind]
+            lead = jnp.sqrt(
+                jnp.maximum(4.0 * degree_real * degree_real - 1.0, 0.0)
+                / jnp.maximum(degree_real * degree_real - squared[kind], 1.0)
+            )
+            back = jnp.sqrt(
+                jnp.maximum(lower * lower - squared[kind], 0.0)
+                / jnp.maximum(4.0 * lower * lower - 1.0, 1.0)
+            )
+            general = lead * (cosine * previous - back * older)
+            first = first_lead[kind] * cosine * previous
+            value = jnp.where(
+                ids[kind] == degree,
+                diagonal[kind],
+                jnp.where(
+                    ids[kind] + 1 == degree,
+                    first,
+                    jnp.where(ids[kind] + 1 < degree, general, 0.0),
+                ),
+            )
+            table[degree, kind * orders : (kind + 1) * orders, :] = value
+            state.append((value, previous))
+        return tuple(state)
+
+    zeros = cosine * 0.0
+    lax.fori_loop(0, degrees, advance, ((zeros, zeros),) * kinds)
 
     def place(slot, carry):
-        value = table[deg_ref[slot]]
-        for half in range(halves):
-            by_slot[half, pl.ds(slot, orders, stride=degrees), :] = value[
-                :, half * LANES : (half + 1) * LANES
-            ]
+        by_slot[pl.ds(slot, every, stride=degrees), :] = table[deg_ref[slot]]
         return carry
 
     lax.fori_loop(0, degrees, place, 0)
-    quadrature = quad_ref[...]
-    for order in range(orders):
-        for half in range(halves):
-            low = half * LANES
-            high = min(lats, low + LANES)
-            chosen = by_slot[half, order * degrees : (order + 1) * degrees, :][:, : high - low]
-            ptab[order, :, low:high] = chosen.astype(jnp.bfloat16)
-            qtab[order, :, low:high] = (chosen * quadrature[:, low:high]).astype(jnp.bfloat16)
+    quadrature = quad_ref[side][:1, :lats]
+    for kind in range(kinds):
+
+        def keep(order, carry):
+            start = pl.multiple_of((kind * orders + order) * degrees, degrees)
+            chosen = by_slot[pl.ds(start, degrees), :][:, :lats]
+            ptab[kind, order] = chosen.astype(jnp.bfloat16)
+            qtab[kind, order] = (chosen * quadrature).astype(jnp.bfloat16)
+            return carry
+
+        lax.fori_loop(0, orders, keep, 0)
 
 
 def pair_swap(values, even_sign):
@@ -271,22 +280,56 @@
     n, nb, fields, cotangent, weights, deg_ref, diag_ref, cos_ref, quad_ref,
     fwd_fk, fwd_kf, inv_fk, inv_kf,
     grad_out, dw_out,
-    fbuf, cbuf, wbuf, band_out, band_in, ord_in, ord_out, deg_out, deg_back, co, go, mixed,
-    wide_a, wide_b, dw, dw_in, qtab, ptab, table, by_slot,
+    fbuf, cbuf, wbuf, band_out, band_in, ord_in, ord_out, cross_out, cross_in, slot_out, slot_all,
+    co, go, mixed, wide_a, wide_b, dw, dw_in, qtab, ptab, table,
     load_sem, send_sem, recv_sem, dw_send, dw_recv, out_sem,
 ):
     me = lax.axis_index("lat")
     me_b = lax.axis_index("batch")
     chunks, lat_dev = fbuf.shape[0], fbuf.shape[1]
-    orders = qtab.shape[0]
+    kinds, orders, degrees, side_lats = qtab.shape
     rows = 2 * orders
     slots = co.shape[1]
-    degrees = n * slots
-    lats = n * lat_dev
+    quarter = n // kinds
+    half = n // 2
+    own = half * slots
+    inner_kinds = ord_in.shape[0]
+    pairs = kinds // 2
+    jobs = kinds * chunks
+    plane_rows = quarter * rows
     mesh_id = pl.DeviceIdType.MESH
+    side = lax.div(me, half)
+    place_in = lax.rem(me, half)
+    column = lax.rem(me, quarter)
+    inner = jnp.where(lax.div(me, quarter) == 1 + side, 1, 0)
+    across = 1 - side
 
     def lanes(chunk):
         return pl.ds(chunk * LANES, LANES)
+
+    def group(kind, at):
+        return jnp.where(
+            lax.rem(kind, 2) == 0, kind * quarter + at, (kind + 1) * quarter - 1 - at
+        )
+
+    def group_rows(kind, at):
+        return pl.ds(pl.multiple_of(group(kind, at) * rows, rows), rows)
+
+    def owner(kind, on_side, at):
+        plane = jnp.where(kind < inner_kinds, 1 + on_side, (kinds - 1) * on_side)
+        return plane * quarter + at
+
+    def mine(kind):
+        return jnp.where(kind < inner_kinds, 1, 0) == inner
+
+    def job_of(job):
+        per_pass = pairs * chunks
+        inside = lax.rem(job, per_pass)
+        kind = lax.div(job, per_pass) * pairs + lax.rem(inside, pairs)
+        return kind, lax.div(inside, pairs), lax.rem(kind, inner_kinds)
+
+    def job_at(kind, chunk):
+        return (kind // pairs) * (pairs * chunks) + chunk * pairs + kind % pairs
 
     def load(chunk):
         return pltpu.make_async_copy(
@@ -318,95 +361,181 @@
         pl.semaphore_signal(barrier, inc=1, device_id={"batch": peer}, device_id_type=mesh_id)
     pl.semaphore_wait(barrier, n - 1 + nb - 1)
 
-    def part(ref, chunk, kind, owner):
-        if kind == "band":
-            return ref.at[chunk, :, pl.ds(pl.multiple_of(owner * rows, rows), rows), :]
-        if kind == "lat":
-            return ref.at[chunk, pl.ds(owner * lat_dev, lat_dev)]
-        return ref.at[chunk, pl.ds(owner * slots, slots)]
-
-    def exchange(stage, chunk, source, source_kind, target, target_kind):
+    def remote(stage, job, source, target, peer):
+        pltpu.make_async_remote_copy(
+            src_ref=source,
+            dst_ref=target,
+            send_sem=send_sem.at[stage, job],
+            recv_sem=recv_sem.at[stage, job],
+            device_id={"lat": peer},
+            device_id_type=mesh_id,
+        ).start()
+
+    def await_bytes(view, sem):
+        pltpu.make_async_copy(view, view, sem).wait()
+
+    def to_owners(stage, kind, chunk, source, target, width):
+        job = job_at(kind, chunk)
+        for step in range(quarter):
+            at = lax.rem(column + step, quarter)
+            view = source.at[chunk, :, group_rows(kind, at), :]
+            spot = target(kind % inner_kinds, chunk)
+            peer = owner(kind, side, at)
+
+            @pl.when(peer != me)
+            def _():
+                remote(stage, job, view, spot, peer)
+
+            @pl.when(peer == me)
+            def _():
+                pltpu.make_async_copy(view, spot, recv_sem.at[stage, job]).start()
+
+    def left_for_owners(stage, kind, chunk, source):
+        job = job_at(kind, chunk)
+
+        @pl.when(mine(kind))
+        def _():
+            await_bytes(source.at[chunk, :, 0 : plane_rows - rows, :], send_sem.at[stage, job])
+
+        @pl.when(jnp.logical_not(mine(kind)))
+        def _():
+            await_bytes(source.at[chunk, :, 0:plane_rows, :], send_sem.at[stage, job])
+
+    def from_owner(stage, job, kind, chunk, source, depth, target):
+        place = lax.rem(kind, inner_kinds)
+        spot = target.at[chunk, :, group_rows(kind, column), :]
+
         def send(step, carry):
-            peer = lax.rem(me + 1 + lax.rem((step - 1) * max(n // 4, 1), n - 1), n)
-            pltpu.make_async_remote_copy(
-                src_ref=part(source, chunk, source_kind, peer),
-                dst_ref=part(target, chunk, target_kind, me),
-                send_sem=send_sem.at[stage, chunk],
-                recv_sem=recv_sem.at[stage, chunk],
-                device_id={"lat": peer},
-                device_id_type=mesh_id,
-            ).start()
-            return carry
-
-        lax.fori_loop(1, n, send, 0)
+            at = lax.rem(place_in + step, half)
+            remote(
+                stage, job, source.at[place, chunk, pl.ds(at * depth, depth)], spot,
+                side * half + at,
+            )
+            return carry
+
+        lax.fori_loop(1, half, send, 0)
         pltpu.make_async_copy(
-            part(source, chunk, source_kind, me),
-            part(target, chunk, target_kind, me),
-            recv_sem.at[stage, chunk],
+            source.at[place, chunk, pl.ds(place_in * depth, depth)], spot, recv_sem.at[stage, job]
         ).start()
 
-    def arrived(stage, chunk, target):
-        pltpu.make_async_copy(target.at[chunk], target.at[chunk], recv_sem.at[stage, chunk]).wait()
-
-    def departed(stage, chunk, source, kind):
-        if kind == "band":
-            view = source.at[chunk, :, 0 : (n - 1) * rows, :]
-        elif kind == "lat":
-            view = source.at[chunk, 0 : (n - 1) * lat_dev]
-        else:
-            view = source.at[chunk, 0 : (n - 1) * slots]
-        pltpu.make_async_copy(view, view, send_sem.at[stage, chunk]).wait()
-
-    def widen(source, chunk, depth):
+    def left_owner(stage, job, kind, chunk, source, depth):
+        view = source.at[lax.rem(kind, inner_kinds), chunk, 0 : (half - 1) * depth]
+        await_bytes(view, send_sem.at[stage, job])
+
+    def reached_all(stage, kind, chunk, target):
+        await_bytes(target.at[chunk, :, 0:plane_rows, :], recv_sem.at[stage, job_at(kind, chunk)])
+
+    def lat_spot(place, chunk):
+        return ord_in.at[place, chunk, pl.ds(place_in * lat_dev, lat_dev)]
+
+    def slot_spot(place, chunk):
+        return slot_all.at[place, chunk, pl.ds(me * slots, slots)]
+
+    def wide_start(job):
+        return pl.multiple_of(lax.rem(job, wide_b.shape[0] // wide_a.shape[0]) * wide_a.shape[0], 8)
+
+    def widen(source, place, chunk, depth, count):
         def one(block, carry):
-            piece = source[chunk, pl.ds(block * depth, depth)].astype(jnp.float32)
+            piece = source[place, chunk, pl.ds(block * depth, depth)].astype(jnp.float32)
             wide_a[pl.ds(pl.multiple_of(block * depth * rows, depth * rows), depth * rows), :] = (
                 piece.reshape(depth * rows, LANES)
             )
             return carry
 
-        lax.fori_loop(0, n, one, 0)
-
-    def narrow(target, chunk, depth):
-        def one(block, carry):
-            start = pl.multiple_of(block * depth * rows, depth * rows)
-            piece = wide_b[pl.ds(start, depth * rows), :]
-            target[chunk, pl.ds(block * depth, depth)] = piece.reshape(
-                depth, rows, LANES
-            ).astype(jnp.bfloat16)
-            return carry
-
-        lax.fori_loop(0, n, one, 0)
-
-    def apply_table(table, depth_in, depth_out, dims):
+        lax.fori_loop(0, count // depth, one, 0)
+
+    def apply_table(tab, kind, start, depth_in, depth_out, dims):
         def one(order, carry):
             real = wide_a[pl.ds(2 * order, depth_in, stride=rows), :]
             imag = wide_a[pl.ds(2 * order + 1, depth_in, stride=rows), :]
             both = jnp.concatenate([real, imag], axis=1).astype(jnp.bfloat16)
-            result = dot(table[order], both, dims)
-            wide_b[pl.ds(2 * order, depth_out, stride=rows), :] = result[:, :LANES]
-            wide_b[pl.ds(2 * order + 1, depth_out, stride=rows), :] = result[:, LANES:]
+            result = dot(tab[kind, order], both, dims)
+            wide_b[pl.ds(start + 2 * order, depth_out, stride=rows), :] = result[:, :LANES]
+            wide_b[pl.ds(start + 2 * order + 1, depth_out, stride=rows), :] = result[:, LANES:]
             return carry
 
         lax.fori_loop(0, orders, one, 0)
 
-    def analyse(stage, chunk, table, target, before):
-        arrived(stage, chunk, ord_in)
-        widen(ord_in, chunk, lat_dev)
-        apply_table(table, lats, degrees, ((1,), (0,)))
-        if before is not None:
-            departed(before, chunk, deg_out, "slot")
-        narrow(deg_out, chunk, slots)
-        exchange(stage + 1, chunk, deg_out, "slot", target, "band")
-
-    def synthesise(stage, chunk, table, before):
-        arrived(stage, chunk, deg_back)
-        widen(deg_back, chunk, slots)
-        apply_table(table, degrees, lats, ((0,), (0,)))
-        if before is not None:
-            departed(before, chunk, ord_out, "lat")
-        narrow(ord_out, chunk, lat_dev)
-        exchange(stage + 1, chunk, ord_out, "lat", band_in, "band")
+    def narrow(target, place, chunk, start, depth, count):
+        def one(block, carry):
+            low = pl.multiple_of(start + block * depth * rows, 8)
+            piece = wide_b[pl.ds(low, depth * rows), :]
+            target[place, chunk, pl.ds(block * depth, depth)] = piece.reshape(
+                depth, rows, LANES
+            ).astype(jnp.bfloat16)
+            return carry
+
+        lax.fori_loop(0, count // depth, one, 0)
+
+    def analyse(base, tab, job):
+        kind, chunk, place = job_of(job)
+
+        @pl.when(mine(kind))
+        def _():
+            await_bytes(ord_in.at[place, chunk], recv_sem.at[base, job])
+            widen(ord_in, place, chunk, lat_dev, side_lats)
+            start = wide_start(job)
+            apply_table(tab, kind, start, side_lats, degrees, ((1,), (0,)))
+            if base:
+                await_bytes(cross_out.at[place, chunk], send_sem.at[1, job])
+            narrow(cross_out, place, chunk, start + across * own * rows, slots, own)
+            remote(
+                base + 1, job, cross_out.at[place, chunk], cross_in.at[place, chunk],
+                owner(kind, across, column),
+            )
+
+    def settle(base, target, job):
+        kind, chunk, place = job_of(job)
+
+        @pl.when(mine(kind))
+        def _():
+            await_bytes(cross_in.at[place, chunk], recv_sem.at[base + 1, job])
+            if base:
+                left_owner(2, job, kind, chunk, slot_out, slots)
+                await_bytes(slot_all.at[place, chunk, 0:own], send_sem.at[4, job])
+            start = wide_start(job) + side * own * rows
+
+            def one(block, carry):
+                low = pl.multiple_of(start + block * slots * rows, 8)
+                piece = wide_b[pl.ds(low, slots * rows), :].reshape(slots, rows, LANES)
+                other = cross_in[place, chunk, pl.ds(block * slots, slots)].astype(jnp.float32)
+                slot_out[place, chunk, pl.ds(block * slots, slots)] = (piece + other).astype(
+                    jnp.bfloat16
+                )
+                return carry
+
+            lax.fori_loop(0, half, one, 0)
+            from_owner(base + 2, job, kind, chunk, slot_out, slots, target)
+
+    def relay(base, job):
+        kind, chunk, place = job_of(job)
+
+        @pl.when(mine(kind))
+        def _():
+            await_bytes(slot_all.at[place, chunk, 0:own], recv_sem.at[base + 3, job])
+            view = slot_all.at[place, chunk, pl.ds(side * own, own)]
+            remote(base + 4, job, view, view, owner(kind, across, column))
+
+    def synthesise(base, tab, job):
+        kind, chunk, place = job_of(job)
+
+        @pl.when(mine(kind))
+        def _():
+            await_bytes(slot_all.at[place, chunk, 0:own], recv_sem.at[base + 4, job])
+            widen(slot_all, place, chunk, slots, degrees)
+            start = wide_start(job)
+            apply_table(tab, kind, start, degrees, side_lats, ((0,), (0,)))
+            if base:
+                left_owner(5, job, kind, chunk, ord_out, lat_dev)
+            narrow(ord_out, place, chunk, start, lat_dev, side_lats)
+            from_owner(base + 5, job, kind, chunk, ord_out, lat_dev, band_in)
+
+    def loop(low, high, body):
+        def one(job, carry):
+            body(job)
+            return carry
+
+        lax.fori_loop(low, high, one, 0)
 
     def pair(source, chunk, row):
         return jnp.concatenate([source[chunk, 2 * row], source[chunk, 2 * row + 1]], axis=1)
@@ -416,8 +545,89 @@
         target[chunk, 2 * row] = values[:, :LANES]
         target[chunk, 2 * row + 1] = values[:, LANES:]
 
-    def joined(source, slot):
-        return jnp.concatenate([source[chunk, slot] for chunk in range(chunks)], axis=1)
+    def joined(source, slot, span):
+        return jnp.concatenate([source[chunk, slot, span] for chunk in range(chunks)], axis=1)
+
+    def mix(part, chunk):
+        low = part * pairs * plane_rows
+        span = slice(low, low + pairs * plane_rows)
+        columns = slice(chunk * LANES, (chunk + 1) * LANES)
+
+        def one(slot, carry):
+            both = dot(
+                joined(co, slot, span),
+                jnp.concatenate([wbuf[slot, 0, :, columns], wbuf[slot, 1, :, columns]], axis=1),
+            )
+            crossed = pair_swap(both[:, LANES:], -1.0)
+            mixed[chunk, slot, span] = (both[:, :LANES] + crossed).astype(jnp.bfloat16)
+            return carry
+
+        return one
+
+    def adjoint(part, chunk):
+        low = part * pairs * plane_rows
+        span = slice(low, low + pairs * plane_rows)
+        columns = slice(chunk * LANES, (chunk + 1) * LANES)
+
+        def one(slot, carry):
+            both = dot(
+                joined(go, slot, span),
+                jnp.concatenate([wbuf[slot, 0, columns, :], wbuf[slot, 1, columns, :]], axis=0),
+                ((1,), (1,)),
+            )
+            crossed = pair_swap(both[:, LANES:], 1.0)
+            mixed[chunk, slot, span] = (both[:, :LANES] + crossed).astype(jnp.bfloat16)
+            return carry
+
+        return one
+
+    def filter_part(base, part, source, make):
+        part_kinds = range(part * pairs, (part + 1) * pairs)
+        for chunk in range(chunks):
+            for kind in part_kinds:
+                reached_all(base + 2, kind, chunk, source)
+        for chunk in range(chunks):
+            if base:
+                for kind in part_kinds:
+                    left_for_owners(3, kind, chunk, mixed)
+            lax.fori_loop(0, slots, make(part, chunk), 0)
+            for kind in part_kinds:
+                to_owners(base + 3, kind, chunk, mixed, slot_spot, slots)
+
+    per_pass = pairs * chunks
+    lag = 2
+
+    def to_filter(base, tab, source, make):
+        loop(0, lag, lambda job: analyse(base, tab, job))
+
+        def step(job):
+            analyse(base, tab, job)
+            settle(base, source, job - lag)
+
+        loop(lag, jobs, step)
+        filter_part(base, 0, source, make)
+        settle(base, source, jobs - lag)
+        loop(0, per_pass, lambda job: relay(base, job))
+        for job in range(jobs - lag + 1, jobs):
+            settle(base, source, job)
+        filter_part(base, 1, source, make)
+
+    def from_filter(base, tab, finish):
+        def step(job):
+            synthesise(base, tab, job)
+            relay(base, job + per_pass)
+
+        loop(0, per_pass, step)
+        for chunk in range(chunks):
+            first = per_pass + chunk * pairs
+            loop(first, first + pairs, lambda job: synthesise(base, tab, job))
+            if chunk:
+                finish(chunk - 1)
+        finish(chunks - 1)
+
+    def spread(stage, chunk, part):
+        for kind in range(part * pairs, (part + 1) * pairs):
+            to_owners(stage, kind, chunk, band_out, lat_spot, lat_dev)
 
     for chunk in range(chunks):
         load(chunk).wait()
@@ -427,35 +637,21 @@
             return carry
 
         lax.fori_loop(0, lat_dev // 2, fourier, 0)
-        exchange(0, chunk, band_out, "band", ord_in, "lat")
+        spread(0, chunk, 0)
+    for chunk in range(chunks):
+        spread(0, chunk, 1)
     fill_tables(
-        me * orders, deg_ref, diag_ref, cos_ref, quad_ref, qtab, ptab, table, by_slot
+        side, [group(kind, column) * orders for kind in range(kinds)], deg_ref, diag_ref, cos_ref,
+        quad_ref, qtab, ptab, table, wide_b,
     )
-    for chunk in range(chunks):
-        analyse(0, chunk, qtab, co, None)
     load_w.wait()
-    for chunk in range(chunks):
-        arrived(1, chunk, co)
-    for chunk in range(chunks):
-
-        def mix(slot, carry):
-            values = joined(co, slot)
-            span = slice(chunk * LANES, (chunk + 1) * LANES)
-            both = dot(
-                values, jnp.concatenate([wbuf[slot, 0, :, span], wbuf[slot, 1, :, span]], axis=1)
-            )
-            crossed = pair_swap(both[:, LANES:], -1.0)
-            mixed[chunk, slot] = (both[:, :LANES] + crossed).astype(jnp.bfloat16)
-            return carry
-
-        lax.fori_loop(0, slots, mix, 0)
-        exchange(2, chunk, mixed, "band", deg_back, "slot")
-    for chunk in range(chunks):
-        synthesise(2, chunk, ptab, None)
-    for chunk in range(chunks):
+    to_filter(0, qtab, co, mix)
+
+    def between(chunk):
         load_cot(chunk).wait()
-        arrived(3, chunk, band_in)
-        departed(0, chunk, band_out, "band")
+        for kind in range(kinds):
+            reached_all(5, kind, chunk, band_in)
+            left_for_owners(0, kind, chunk, band_out)
 
         def middle(row, carry):
             response = dot(inv_kf[...], pair(band_in, chunk, row))
@@ -464,32 +660,16 @@
             return carry
 
         lax.fori_loop(0, lat_dev // 2, middle, 0)
-        exchange(4, chunk, band_out, "band", ord_in, "lat")
+        spread(6, chunk, 0)
+
+    from_filter(0, ptab, between)
     for chunk in range(chunks):
-        analyse(4, chunk, ptab, go, 1)
-    for chunk in range(chunks):
-        arrived(5, chunk, go)
-    for chunk in range(chunks):
-        departed(2, chunk, mixed, "band")
-
-        def adjoint(slot, carry):
-            values = joined(go, slot)
-            span = slice(chunk * LANES, (chunk + 1) * LANES)
-            both = dot(
-                values,
-                jnp.concatenate([wbuf[slot, 0, span, :], wbuf[slot, 1, span, :]], axis=0),
-                ((1,), (1,)),
-            )
-            crossed = pair_swap(both[:, LANES:], 1.0)
-            mixed[chunk, slot] = (both[:, :LANES] + crossed).astype(jnp.bfloat16)
-            return carry
-
-        lax.fori_loop(0, slots, adjoint, 0)
-        exchange(6, chunk, mixed, "band", deg_back, "slot")
+        spread(6, chunk, 1)
+    to_filter(6, ptab, go, adjoint)
 
     def weight_grad(slot, carry):
-        values = joined(co, slot)
-        grads = joined(go, slot)
+        values = joined(co, slot, slice(None))
+        grads = joined(go, slot, slice(None))
         turned = pair_swap(grads.astype(jnp.float32), 1.0).astype(jnp.bfloat16)
         span = ((0,), (0,))
         dw[slot, 0] = dot(values, grads, span).astype(jnp.bfloat16)
@@ -510,10 +690,13 @@
         )
         copy.start()
         dw_copies.append(copy)
-    for chunk in range(chunks):
-        synthesise(6, chunk, qtab, 3)
-    for copy in dw_copies:
-        copy.wait()
+
+    def store(chunk):
+        return pltpu.make_async_copy(
+            cbuf.at[chunk], grad_out.at[0, :, :, lanes(chunk)], out_sem.at[chunk]
+        )
+
+    store_w = pltpu.make_async_copy(dw, dw_out, out_sem.at[chunks])
 
     def total(slot, carry):
         value = dw[slot].astype(jnp.float32)
@@ -522,17 +705,14 @@
         dw[slot] = value.astype(jnp.bfloat16)
         return carry
 
-    lax.fori_loop(0, slots, total, 0)
-    store_w = pltpu.make_async_copy(dw, dw_out, out_sem.at[chunks])
-    store_w.start()
-
-    def store(chunk):
-        return pltpu.make_async_copy(
-            cbuf.at[chunk], grad_out.at[0, :, :, lanes(chunk)], out_sem.at[chunk]
-        )
-
-    for chunk in range(chunks):
-        arrived(7, chunk, band_in)
+    def last(chunk):
+        if chunk == 0:
+            for copy in dw_copies:
+                copy.wait()
+            lax.fori_loop(0, slots, total, 0)
+            store_w.start()
+        for kind in range(kinds):
+            reached_all(11, kind, chunk, band_in)
 
         def finish(row, carry):
             delta = dot(fwd_kf[...], pair(band_in, chunk, row))
@@ -541,27 +721,42 @@
 
         lax.fori_loop(0, lat_dev // 2, finish, 0)
         store(chunk).start()
+
+    from_filter(6, qtab, last)
     for chunk in range(chunks):
-        departed(4, chunk, band_out, "band")
-        departed(5, chunk, deg_out, "slot")
-        departed(6, chunk, mixed, "band")
-        departed(7, chunk, ord_out, "lat")
+        for kind in range(kinds):
+            left_for_owners(6, kind, chunk, band_out)
+            left_for_owners(9, kind, chunk, mixed)
+
+    def drain(job):
+        kind, chunk, place = job_of(job)
+
+        @pl.when(mine(kind))
+        def _():
+            await_bytes(cross_out.at[place, chunk], send_sem.at[7, job])
+            left_owner(8, job, kind, chunk, slot_out, slots)
+            await_bytes(slot_all.at[place, chunk, 0:own], send_sem.at[10, job])
+            left_owner(11, job, kind, chunk, ord_out, lat_dev)
+
+    loop(0, jobs, drain)
+    for chunk in range(chunks):
         store(chunk).wait()
     store_w.wait()
 
 
 def local_kernel(fields, cotangent, weights, degree_of):
-    if fields.shape[0] != 1 or fields.shape[1] % 2:
-        return local(fields, cotangent, weights, degree_of)
     n = lax.axis_size("lat")
     nb = lax.axis_size("batch")
+    kinds = 4
+    if fields.shape[0] != 1 or fields.shape[1] % 2 or n % kinds or ORDERS != n * GROUP:
+        return local(fields, cotangent, weights, degree_of)
     lat_dev, lons, channels = fields.shape[1:]
     slots = weights.shape[0]
-    orders = ORDERS // n
-    rows = 2 * orders
+    rows = 2 * GROUP
     chunks = channels // LANES
-    floats, waves = constant_tables(orders)
-    halves = -(-LATS // LANES)
+    floats, waves = constant_tables()
+    side_lats = LATS // 2
+    held = kinds - 1
     vmem = pl.BlockSpec(memory_space=pltpu.VMEM)
     anywhere = pl.BlockSpec(memory_space=pl.ANY)
 
@@ -570,7 +765,7 @@
 
     dma = pltpu.SemaphoreType.DMA
     others = max(nb - 1, 1)
-    wide_rows = max(LATS, DEGREES) * rows
+    wide_rows = max(side_lats, DEGREES) * rows
     return pl.pallas_call(
         functools.partial(block_kernel, n, nb),
         out_shape=(
@@ -585,30 +780,31 @@
             buffer(*weights.shape),
             buffer(chunks, lat_dev, n * rows, LANES),
             buffer(chunks, lat_dev, n * rows, LANES),
-            buffer(chunks, LATS, rows, LANES),
-            buffer(chunks, LATS, rows, LANES),
-            buffer(chunks, DEGREES, rows, LANES),
-            buffer(chunks, DEGREES, rows, LANES),
+            buffer(held, chunks, side_lats, rows, LANES),
+            buffer(held, chunks, side_lats, rows, LANES),
+            buffer(held, chunks, DEGREES // 2, rows, LANES),
+            buffer(held, chunks, DEGREES // 2, rows, LANES),
+            buffer(held, chunks, DEGREES // 2, rows, LANES),
+            buffer(held, chunks, DEGREES, rows, LANES),
             buffer(chunks, slots, n * rows, LANES),
             buffer(chunks, slots, n * rows, LANES),
             buffer(chunks, slots, n * rows, LANES),
             pltpu.VMEM((wide_rows, LANES), jnp.float32),
-            pltpu.VMEM((wide_rows, LANES), jnp.float32),
+            pltpu.VMEM((3 * wide_rows, LANES), jnp.float32),
             buffer(*weights.shape),
             buffer(others, *weights.shape),
-            buffer(orders, DEGREES, LATS),
-            buffer(orders, DEGREES, LATS),
-            pltpu.VMEM((DEGREES, orders, halves * LANES), jnp.float32),
-            pltpu.VMEM((halves, orders * DEGREES, LANES), jnp.float32),
+            buffer(kinds, GROUP, DEGREES, side_lats),
+            buffer(kinds, GROUP, DEGREES, side_lats),
+            pltpu.VMEM((DEGREES, kinds * GROUP, LANES), jnp.float32),
             dma((2 * chunks + 1,)),
-            dma((8, chunks)),
-            dma((8, chunks)),
+            dma((12, kinds * chunks)),
+            dma((12, kinds * chunks)),
             dma((others,)),
             dma((others,)),
             dma((chunks + 1,)),
         ],
         compiler_params=pltpu.CompilerParams(
-            collective_id=0, has_side_effects=True, vmem_limit_bytes=60 * 2**20
+            collective_id=0, has_side_effects=True, vmem_limit_bytes=63 * 2**20
         ),
         name="filter_block",
     )(
@@ -654,9 +850,8 @@
 
 
 def solution(mesh):
-    orders = ORDERS // mesh.shape["lat"]
     return jax.shard_map(
-        local_kernel if orders % 8 == 0 and CHANNELS % LANES == 0 else local,
+        local_kernel if CHANNELS % LANES == 0 else local,
         mesh=mesh,
         in_specs=(
             P("batch", "lat", None, None),

time: 364 us -> 338 us (0.929)
  Pallas kernels: 357 us -> 331 us
    pallas_call x1, Pallas kernels: 357 us -> 331 us  [local_kernel(): pl.pallas_call(functools.partial(block_kernel, n, nb), out_shape=(jax.Sha...]
where the time goes in v1:
time: 338 us
  Pallas kernels  331 us (98%)
  local copies, waits for them, and re-layouts  6.5 us (2%)
    pallas_call x1, Pallas kernels, local_kernel(): pl.pallas_call(functools.partial(block_kernel, n, nb), out_shape=(jax.Sha...  331 us

profile of v1, /device:TPU:0, one launch (start us, length us, event | category | flops | bytes accessed | tf_op | source)
XLA Modules:
  0.0 338.2 jit_solution(13676355825409256865)
XLA Ops:
  0.6 331.1 %filter_block.1 = (bf16[1,12,384,384]{3,2,1,0:T(8,128)(2,1)}, bf16[8,2,384,384]{3,2,1,0:T(8,128)(2,1)}) custom-call(bf16[1,12,384,384]{3,2,1,0:T(8,128)(2,1)} %fields.1, bf16[1,12,384,384]{3,2,1,0:T(8,128)(2,1)} %cotangent.1, bf16[8,2,384,384]{3,2,1,0:T(8,128)(2,1)} %weights.1, s32[128]{0:T(128)} %deg_ref.1, f32[2,128,128]{2,1,0:T(8,128)} %constant.14.clone.diag_ref, ...), custom_call_target="tpu_custom_call" | custom-call | tf_op jit(solution)/shard_map/filter_block/pallas_call | solution.py:769
  331.7 0.0 copy-start
  331.7 4.3 %copy.15 = bf16[1,12,384,384]{3,2,1,0:T(8,128)(2,1)} copy(bf16[1,12,384,384]{3,2,1,0:T(8,128)(2,1)} %get-tuple-element.4) | data formatting | bytes 7077888
  336.0 0.0 copy-done
  336.0 2.2 copy.16
Async XLA Ops:
  331.7 4.3 %copy-start = (bf16[8,2,384,384]{3,2,1,0:T(8,128)(2,1)S(1)}, bf16[8,2,384,384]{3,2,1,0:T(8,128)(2,1)}, u32[]{:S(2)}) copy-start(bf16[8,2,384,384]{3,2,1,0:T(8,128)(2,1)} %get-tuple-element.5) | copy-start | bytes 14155780

commit v2 on v1

--- a/solution.py
+++ b/solution.py
@@ -239,19 +239,30 @@
     zeros = cosine * 0.0
     lax.fori_loop(0, degrees, advance, ((zeros, zeros),) * kinds)
 
+    ahead = every // 2
+    tail = degrees // 2
+
     def place(slot, carry):
-        by_slot[pl.ds(slot, every, stride=degrees), :] = table[deg_ref[slot]]
+        by_slot[pl.ds(slot, ahead, stride=degrees), :] = table[deg_ref[slot], :ahead]
         return carry
 
-    lax.fori_loop(0, degrees, place, 0)
+    lax.fori_loop(0, degrees, place, 0, unroll=4)
+
+    def place_tail(row, carry):
+        spots = pl.ds(ahead * degrees + row, ahead, stride=degrees)
+        by_slot[spots, :] = table[tail + row, ahead:]
+        return carry
+
+    lax.fori_loop(0, tail, place_tail, 0, unroll=4)
     quadrature = quad_ref[side][:1, :lats]
     for kind in range(kinds):
 
         def keep(order, carry):
             start = pl.multiple_of((kind * orders + order) * degrees, degrees)
-            chosen = by_slot[pl.ds(start, degrees), :][:, :lats]
-            ptab[kind, order] = chosen.astype(jnp.bfloat16)
-            qtab[kind, order] = (chosen * quadrature).astype(jnp.bfloat16)
+            depth = degrees if kind < kinds // 2 else tail
+            chosen = by_slot[pl.ds(start, depth), :][:, :lats]
+            ptab[kind, order, :depth] = chosen.astype(jnp.bfloat16)
+            qtab[kind, order, :depth] = (chosen * quadrature).astype(jnp.bfloat16)
             return carry
 
         lax.fori_loop(0, orders, keep, 0)
@@ -281,7 +292,7 @@
     fwd_fk, fwd_kf, inv_fk, inv_kf,
     grad_out, dw_out,
     fbuf, cbuf, wbuf, band_out, band_in, ord_in, ord_out, cross_out, cross_in, slot_out, slot_all,
-    co, go, mixed, wide_a, wide_b, dw, dw_in, qtab, ptab, table,
+    tail_out, co, go, mixed, wide_a, wide_b, dw, dw_in, qtab, ptab, table, row_ref, slot_of, by_name,
     load_sem, send_sem, recv_sem, dw_send, dw_recv, out_sem,
 ):
     me = lax.axis_index("lat")
@@ -328,6 +339,23 @@
         kind = lax.div(job, per_pass) * pairs + lax.rem(inside, pairs)
         return kind, lax.div(inside, pairs), lax.rem(kind, inner_kinds)
 
+    def first_block(kind):
+        return group(kind, column) - own // orders
+
+    def tail_blocks(kind, body):
+        def one(block, carry):
+            body(pl.multiple_of(block * orders, orders))
+            return carry
+
+        lax.fori_loop(first_block(kind), own // orders, one, 0)
+
+    def await_tail(kind, view, sem):
+        for first in range(own // orders):
+
+            @pl.when(first_block(kind) == first)
+            def _():
+                await_bytes(view.at[pl.ds(0, own - first * orders)], sem)
+
     def job_at(kind, chunk):
         return (kind // pairs) * (pairs * chunks) + chunk * pairs + kind % pairs
 
@@ -444,12 +472,12 @@
 
         lax.fori_loop(0, count // depth, one, 0)
 
-    def apply_table(tab, kind, start, depth_in, depth_out, dims):
+    def apply_table(tab, kind, kept, start, depth_in, depth_out, dims):
         def one(order, carry):
             real = wide_a[pl.ds(2 * order, depth_in, stride=rows), :]
             imag = wide_a[pl.ds(2 * order + 1, depth_in, stride=rows), :]
             both = jnp.concatenate([real, imag], axis=1).astype(jnp.bfloat16)
-            result = dot(tab[kind, order], both, dims)
+            result = dot(tab[kind, order, :kept], both, dims)
             wide_b[pl.ds(start + 2 * order, depth_out, stride=rows), :] = result[:, :LANES]
             wide_b[pl.ds(start + 2 * order + 1, depth_out, stride=rows), :] = result[:, LANES:]
             return carry
@@ -467,7 +495,19 @@
 
         lax.fori_loop(0, count // depth, one, 0)
 
-    def analyse(base, tab, job):
+    def wide_rows(start, index, depth):
+        return pl.ds(pl.multiple_of(start + index * rows, 8), depth * rows)
+
+    def blank(first, count):
+        def one(block, carry):
+            by_name[pl.ds((first + block) * orders, orders)] = jnp.zeros(
+                (orders, rows, LANES), jnp.bfloat16
+            )
+            return carry
+
+        lax.fori_loop(0, count, one, 0)
+
+    def analyse(base, tab, part, job):
         kind, chunk, place = job_of(job)
 
         @pl.when(mine(kind))
@@ -475,56 +515,137 @@
             await_bytes(ord_in.at[place, chunk], recv_sem.at[base, job])
             widen(ord_in, place, chunk, lat_dev, side_lats)
             start = wide_start(job)
-            apply_table(tab, kind, start, side_lats, degrees, ((1,), (0,)))
+            peer = owner(kind, across, column)
+            source = cross_out.at[place, chunk]
+            target = cross_in.at[place, chunk]
+            kept = own if part else degrees
+            apply_table(tab, kind, kept, start, side_lats, kept, ((1,), (0,)))
+            if not part:
+                if base:
+                    await_bytes(source, send_sem.at[1, job])
+                narrow(cross_out, place, chunk, start + across * own * rows, slots, own)
+                remote(base + 1, job, source, target, peer)
+                return
             if base:
-                await_bytes(cross_out.at[place, chunk], send_sem.at[1, job])
-            narrow(cross_out, place, chunk, start + across * own * rows, slots, own)
-            remote(
-                base + 1, job, cross_out.at[place, chunk], cross_in.at[place, chunk],
-                owner(kind, across, column),
-            )
-
-    def settle(base, target, job):
+                await_tail(kind, source, send_sem.at[1, job])
+
+            def send(low):
+                span = pl.ds(low, orders)
+                piece = wide_b[wide_rows(start, low, orders), :]
+                cross_out[place, chunk, span] = piece.reshape(orders, rows, LANES).astype(
+                    jnp.bfloat16
+                )
+                remote(base + 1, job, source.at[span], target.at[span], peer)
+
+            tail_blocks(kind, send)
+
+    def settle(base, target, part, job):
         kind, chunk, place = job_of(job)
 
         @pl.when(mine(kind))
         def _():
-            await_bytes(cross_in.at[place, chunk], recv_sem.at[base + 1, job])
+            start = wide_start(job)
+            if part:
+                await_tail(kind, cross_in.at[place, chunk], recv_sem.at[base + 1, job])
+            else:
+                await_bytes(cross_in.at[place, chunk], recv_sem.at[base + 1, job])
             if base:
                 left_owner(2, job, kind, chunk, slot_out, slots)
-                await_bytes(slot_all.at[place, chunk, 0:own], send_sem.at[4, job])
-            start = wide_start(job) + side * own * rows
-
-            def one(block, carry):
-                low = pl.multiple_of(start + block * slots * rows, 8)
-                piece = wide_b[pl.ds(low, slots * rows), :].reshape(slots, rows, LANES)
-                other = cross_in[place, chunk, pl.ds(block * slots, slots)].astype(jnp.float32)
-                slot_out[place, chunk, pl.ds(block * slots, slots)] = (piece + other).astype(
-                    jnp.bfloat16
-                )
-                return carry
-
-            lax.fori_loop(0, half, one, 0)
+                if part:
+                    await_tail(kind, tail_out.at[chunk], send_sem.at[4, job])
+                else:
+                    await_bytes(slot_all.at[place, chunk, 0:own], send_sem.at[4, job])
+            if part:
+
+                blank(0, own // orders + first_block(kind))
+
+                def add(low):
+                    piece = wide_b[wide_rows(start, low, orders), :]
+                    other = cross_in[place, chunk, pl.ds(low, orders)].astype(jnp.float32)
+                    by_name[pl.ds(own + low, orders)] = (
+                        piece.reshape(orders, rows, LANES) + other
+                    ).astype(jnp.bfloat16)
+
+                tail_blocks(kind, add)
+
+                def pick(slot, carry):
+                    slot_out[place, chunk, slot] = by_name[deg_ref[side * own + slot]]
+                    return carry
+
+                lax.fori_loop(0, own, pick, 0, unroll=4)
+            else:
+
+                def one(block, carry):
+                    low = block * slots
+                    piece = wide_b[wide_rows(start + side * own * rows, low, slots), :]
+                    other = cross_in[place, chunk, pl.ds(low, slots)].astype(jnp.float32)
+                    slot_out[place, chunk, pl.ds(low, slots)] = (
+                        piece.reshape(slots, rows, LANES) + other
+                    ).astype(jnp.bfloat16)
+                    return carry
+
+                lax.fori_loop(0, half, one, 0)
             from_owner(base + 2, job, kind, chunk, slot_out, slots, target)
 
-    def relay(base, job):
+    def relay(base, part, job):
         kind, chunk, place = job_of(job)
 
         @pl.when(mine(kind))
         def _():
             await_bytes(slot_all.at[place, chunk, 0:own], recv_sem.at[base + 3, job])
+            peer = owner(kind, across, column)
             view = slot_all.at[place, chunk, pl.ds(side * own, own)]
-            remote(base + 4, job, view, view, owner(kind, across, column))
-
-    def synthesise(base, tab, job):
+            if not part:
+                remote(base + 4, job, view, view, peer)
+                return
+
+            blank(across * (own // orders), own // orders)
+
+            def copy(block, carry):
+                span = pl.ds(side * own + block * slots, slots)
+                by_name[span] = slot_all[place, chunk, span]
+                return carry
+
+            lax.fori_loop(0, half, copy, 0)
+
+            def send(low):
+                for step in range(orders):
+                    tail_out[chunk, low + step] = by_name[slot_of[0, own + low + step]]
+                span = pl.ds(low, orders)
+                remote(base + 4, job, tail_out.at[chunk, span], view.at[span], peer)
+
+            tail_blocks(kind, send)
+
+    def synthesise(base, tab, part, job):
         kind, chunk, place = job_of(job)
 
         @pl.when(mine(kind))
         def _():
-            await_bytes(slot_all.at[place, chunk, 0:own], recv_sem.at[base + 4, job])
-            widen(slot_all, place, chunk, slots, degrees)
             start = wide_start(job)
-            apply_table(tab, kind, start, degrees, side_lats, ((0,), (0,)))
+            if part:
+                await_tail(kind, tail_out.at[chunk], recv_sem.at[base + 4, job])
+
+                def clear(block, carry):
+                    wide_a[wide_rows(0, block * orders, orders), :] = jnp.zeros(
+                        (orders * rows, LANES), jnp.float32
+                    )
+                    return carry
+
+                lax.fori_loop(0, first_block(kind), clear, 0)
+
+                def add(low):
+                    near = tail_out[chunk, pl.ds(low, orders)].astype(jnp.float32)
+                    far = slot_all[place, chunk, pl.ds(across * own + low, orders)]
+                    wide_a[wide_rows(0, low, orders), :] = (
+                        near + far.astype(jnp.float32)
+                    ).reshape(orders * rows, LANES)
+
+                tail_blocks(kind, add)
+                apply_table(tab, kind, own, start, own, side_lats, ((0,), (0,)))
+            else:
+                await_bytes(slot_all.at[place, chunk, 0:own], recv_sem.at[base + 4, job])
+                widen(slot_all, place, chunk, slots, degrees)
+                apply_table(tab, kind, degrees, start, degrees, side_lats, ((0,), (0,)))
             if base:
                 left_owner(5, job, kind, chunk, ord_out, lat_dev)
             narrow(ord_out, place, chunk, start, lat_dev, side_lats)
@@ -598,29 +719,35 @@
     lag = 2
 
     def to_filter(base, tab, source, make):
-        loop(0, lag, lambda job: analyse(base, tab, job))
-
-        def step(job):
-            analyse(base, tab, job)
-            settle(base, source, job - lag)
-
-        loop(lag, jobs, step)
+        for low, high, part, behind in (
+            (0, lag, 0, None),
+            (lag, per_pass, 0, 0),
+            (per_pass, per_pass + lag, 1, 0),
+            (per_pass + lag, jobs, 1, 1),
+        ):
+
+            def step(job):
+                analyse(base, tab, part, job)
+                if behind is not None:
+                    settle(base, source, behind, job - lag)
+
+            loop(low, high, step)
         filter_part(base, 0, source, make)
-        settle(base, source, jobs - lag)
-        loop(0, per_pass, lambda job: relay(base, job))
+        settle(base, source, 1, jobs - lag)
+        loop(0, per_pass, lambda job: relay(base, 0, job))
         for job in range(jobs - lag + 1, jobs):
-            settle(base, source, job)
+            settle(base, source, 1, job)
         filter_part(base, 1, source, make)
 
     def from_filter(base, tab, finish):
         def step(job):
-            synthesise(base, tab, job)
-            relay(base, job + per_pass)
+            synthesise(base, tab, 0, job)
+            relay(base, 1, job + per_pass)
 
         loop(0, per_pass, step)
         for chunk in range(chunks):
             first = per_pass + chunk * pairs
-            loop(first, first + pairs, lambda job: synthesise(base, tab, job))
+            loop(first, first + pairs, lambda job: synthesise(base, tab, 1, job))
             if chunk:
                 finish(chunk - 1)
         finish(chunks - 1)
@@ -644,6 +771,15 @@
         side, [group(kind, column) * orders for kind in range(kinds)], deg_ref, diag_ref, cos_ref,
         quad_ref, qtab, ptab, table, wide_b,
     )
+    spots = lax.broadcasted_iota(jnp.int32, row_ref.shape, 1)
+
+    def invert(slot, carry):
+        return jnp.where(spots == deg_ref[slot], slot, carry)
+
+    row_ref[...] = lax.fori_loop(0, degrees, invert, spots * 0, unroll=4)
+    turn = pltpu.make_async_copy(row_ref, slot_of, load_sem.at[2 * chunks + 1])
+    turn.start()
+    turn.wait()
     load_w.wait()
     to_filter(0, qtab, co, mix)
 
@@ -728,17 +864,22 @@
             left_for_owners(6, kind, chunk, band_out)
             left_for_owners(9, kind, chunk, mixed)
 
-    def drain(job):
+    def drain(part, job):
         kind, chunk, place = job_of(job)
 
         @pl.when(mine(kind))
         def _():
-            await_bytes(cross_out.at[place, chunk], send_sem.at[7, job])
+            if part:
+                await_tail(kind, cross_out.at[place, chunk], send_sem.at[7, job])
+                await_tail(kind, tail_out.at[chunk], send_sem.at[10, job])
+            else:
+                await_bytes(cross_out.at[place, chunk], send_sem.at[7, job])
+                await_bytes(slot_all.at[place, chunk, 0:own], send_sem.at[10, job])
             left_owner(8, job, kind, chunk, slot_out, slots)
-            await_bytes(slot_all.at[place, chunk, 0:own], send_sem.at[10, job])
             left_owner(11, job, kind, chunk, ord_out, lat_dev)
 
-    loop(0, jobs, drain)
+    loop(0, per_pass, lambda job: drain(0, job))
+    loop(per_pass, jobs, lambda job: drain(1, job))
     for chunk in range(chunks):
         store(chunk).wait()
     store_w.wait()
@@ -786,6 +927,7 @@
             buffer(held, chunks, DEGREES // 2, rows, LANES),
             buffer(held, chunks, DEGREES // 2, rows, LANES),
             buffer(held, chunks, DEGREES, rows, LANES),
+            buffer(chunks, DEGREES // 2, rows, LANES),
             buffer(chunks, slots, n * rows, LANES),
             buffer(chunks, slots, n * rows, LANES),
             buffer(chunks, slots, n * rows, LANES),
@@ -796,7 +938,10 @@
             buffer(kinds, GROUP, DEGREES, side_lats),
             buffer(kinds, GROUP, DEGREES, side_lats),
             pltpu.VMEM((DEGREES, kinds * GROUP, LANES), jnp.float32),
-            dma((2 * chunks + 1,)),
+            pltpu.VMEM((GROUP, DEGREES), jnp.int32),
+            pltpu.SMEM((GROUP, DEGREES), jnp.int32),
+            buffer(DEGREES, rows, LANES),
+            dma((2 * chunks + 2,)),
             dma((12, kinds * chunks)),
             dma((12, kinds * chunks)),
             dma((others,)),

time: 338 us -> 290 us (0.86)
  Pallas kernels: 331 us -> 283 us
    pallas_call x1, Pallas kernels: 331 us -> 283 us  [local_kernel(): pl.pallas_call(functools.partial(block_kernel, n, nb), out_shape=(jax.Sha...]
where the time goes in v2:
time: 290 us
  Pallas kernels  283 us (98%)
  local copies, waits for them, and re-layouts  6.5 us (2%)
    pallas_call x1, Pallas kernels, local_kernel(): pl.pallas_call(functools.partial(block_kernel, n, nb), out_shape=(jax.Sha...  283 us
    unnamed x4, local copies, waits for them, and re-layouts  6.5 us

profile of v2, /device:TPU:0, one launch (start us, length us, event | category | flops | bytes accessed | tf_op | source)
XLA Modules:
  0.0 290.0 jit_solution(9310126722662610269)
XLA Ops:
  0.6 282.9 %filter_block.1 = (bf16[1,12,384,384]{3,2,1,0:T(8,128)(2,1)}, bf16[8,2,384,384]{3,2,1,0:T(8,128)(2,1)}) custom-call(bf16[1,12,384,384]{3,2,1,0:T(8,128)(2,1)} %fields.1, bf16[1,12,384,384]{3,2,1,0:T(8,128)(2,1)} %cotangent.1, bf16[8,2,384,384]{3,2,1,0:T(8,128)(2,1)} %weights.1, s32[128]{0:T(128)} %deg_ref.1, f32[2,128,128]{2,1,0:T(8,128)} %constant.14.clone.diag_ref, ...), custom_call_target="tpu_custom_call" | custom-call | tf_op jit(solution)/shard_map/filter_block/pallas_call | solution.py:910
  283.5 0.0 copy-start
  283.5 4.3 %copy.15 = bf16[1,12,384,384]{3,2,1,0:T(8,128)(2,1)} copy(bf16[1,12,384,384]{3,2,1,0:T(8,128)(2,1)} %get-tuple-element.4) | data formatting | bytes 7077888
  287.8 0.0 copy-done
  287.8 2.2 copy.16
Async XLA Ops:
  283.5 4.3 %copy-start = (bf16[8,2,384,384]{3,2,1,0:T(8,128)(2,1)S(1)}, bf16[8,2,384,384]{3,2,1,0:T(8,128)(2,1)}, u32[]{:S(2)}) copy-start(bf16[8,2,384,384]{3,2,1,0:T(8,128)(2,1)} %get-tuple-element.5) | copy-start | bytes 14155780

commit v3 on v2

--- a/solution.py
+++ b/solution.py
@@ -292,7 +292,7 @@
     fwd_fk, fwd_kf, inv_fk, inv_kf,
     grad_out, dw_out,
     fbuf, cbuf, wbuf, band_out, band_in, ord_in, ord_out, cross_out, cross_in, slot_out, slot_all,
-    tail_out, co, go, mixed, wide_a, wide_b, dw, dw_in, qtab, ptab, table, row_ref, slot_of, by_name,
+    tail_out, co, go, mixed, wide_a, wide_b, wide_c, dw, dw_in, qtab, ptab, table, row_ref, slot_of, by_name,
     load_sem, send_sem, recv_sem, dw_send, dw_recv, out_sem,
 ):
     me = lax.axis_index("lat")
@@ -387,7 +387,6 @@
     for step in range(1, nb):
         peer = lax.rem(me_b + step, nb)
         pl.semaphore_signal(barrier, inc=1, device_id={"batch": peer}, device_id_type=mesh_id)
-    pl.semaphore_wait(barrier, n - 1 + nb - 1)
 
     def remote(stage, job, source, target, peer):
         pltpu.make_async_remote_copy(
@@ -459,8 +458,12 @@
     def slot_spot(place, chunk):
         return slot_all.at[place, chunk, pl.ds(me * slots, slots)]
 
-    def wide_start(job):
-        return pl.multiple_of(lax.rem(job, wide_b.shape[0] // wide_a.shape[0]) * wide_a.shape[0], 8)
+    def wide_start(part, job):
+        if part:
+            spot = lax.rem(lax.div(job - pairs * chunks, pairs) + pairs, chunks)
+        else:
+            spot = jnp.where(job < 2 * pairs, lax.rem(job, pairs), job - pairs)
+        return pl.multiple_of(spot * wide_a.shape[0], 8)
 
     def widen(source, place, chunk, depth, count):
         def one(block, carry):
@@ -472,22 +475,22 @@
 
         lax.fori_loop(0, count // depth, one, 0)
 
-    def apply_table(tab, kind, kept, start, depth_in, depth_out, dims):
+    def apply_table(tab, kind, kept, result_ref, start, depth_in, depth_out, dims):
         def one(order, carry):
             real = wide_a[pl.ds(2 * order, depth_in, stride=rows), :]
             imag = wide_a[pl.ds(2 * order + 1, depth_in, stride=rows), :]
             both = jnp.concatenate([real, imag], axis=1).astype(jnp.bfloat16)
             result = dot(tab[kind, order, :kept], both, dims)
-            wide_b[pl.ds(start + 2 * order, depth_out, stride=rows), :] = result[:, :LANES]
-            wide_b[pl.ds(start + 2 * order + 1, depth_out, stride=rows), :] = result[:, LANES:]
+            result_ref[pl.ds(start + 2 * order, depth_out, stride=rows), :] = result[:, :LANES]
+            result_ref[pl.ds(start + 2 * order + 1, depth_out, stride=rows), :] = result[:, LANES:]
             return carry
 
         lax.fori_loop(0, orders, one, 0)
 
-    def narrow(target, place, chunk, start, depth, count):
+    def narrow(source, target, place, chunk, start, depth, count):
         def one(block, carry):
             low = pl.multiple_of(start + block * depth * rows, 8)
-            piece = wide_b[pl.ds(low, depth * rows), :]
+            piece = source[pl.ds(low, depth * rows), :]
             target[place, chunk, pl.ds(block * depth, depth)] = piece.reshape(
                 depth, rows, LANES
             ).astype(jnp.bfloat16)
@@ -514,16 +517,16 @@
         def _():
             await_bytes(ord_in.at[place, chunk], recv_sem.at[base, job])
             widen(ord_in, place, chunk, lat_dev, side_lats)
-            start = wide_start(job)
+            start = wide_start(part, job)
             peer = owner(kind, across, column)
             source = cross_out.at[place, chunk]
             target = cross_in.at[place, chunk]
             kept = own if part else degrees
-            apply_table(tab, kind, kept, start, side_lats, kept, ((1,), (0,)))
+            apply_table(tab, kind, kept, wide_b, start, side_lats, kept, ((1,), (0,)))
             if not part:
                 if base:
                     await_bytes(source, send_sem.at[1, job])
-                narrow(cross_out, place, chunk, start + across * own * rows, slots, own)
+                narrow(wide_b, cross_out, place, chunk, start + across * own * rows, slots, own)
                 remote(base + 1, job, source, target, peer)
                 return
             if base:
@@ -544,7 +547,7 @@
 
         @pl.when(mine(kind))
         def _():
-            start = wide_start(job)
+            start = wide_start(part, job)
             if part:
                 await_tail(kind, cross_in.at[place, chunk], recv_sem.at[base + 1, job])
             else:
@@ -621,7 +624,6 @@
 
         @pl.when(mine(kind))
         def _():
-            start = wide_start(job)
             if part:
                 await_tail(kind, tail_out.at[chunk], recv_sem.at[base + 4, job])
 
@@ -641,14 +643,14 @@
                     ).reshape(orders * rows, LANES)
 
                 tail_blocks(kind, add)
-                apply_table(tab, kind, own, start, own, side_lats, ((0,), (0,)))
+                apply_table(tab, kind, own, wide_c, 0, own, side_lats, ((0,), (0,)))
             else:
                 await_bytes(slot_all.at[place, chunk, 0:own], recv_sem.at[base + 4, job])
                 widen(slot_all, place, chunk, slots, degrees)
-                apply_table(tab, kind, degrees, start, degrees, side_lats, ((0,), (0,)))
+                apply_table(tab, kind, degrees, wide_c, 0, degrees, side_lats, ((0,), (0,)))
             if base:
                 left_owner(5, job, kind, chunk, ord_out, lat_dev)
-            narrow(ord_out, place, chunk, start, lat_dev, side_lats)
+            narrow(wide_c, ord_out, place, chunk, 0, lat_dev, side_lats)
             from_owner(base + 5, job, kind, chunk, ord_out, lat_dev, band_in)
 
     def loop(low, high, body):
@@ -716,61 +718,61 @@
                 to_owners(base + 3, kind, chunk, mixed, slot_spot, slots)
 
     per_pass = pairs * chunks
-    lag = 2
-
-    def to_filter(base, tab, source, make):
+    def unit(part, chunk):
+        first = part * per_pass + chunk * pairs
+        return first, first + pairs
+
+    def run(spans, body):
+        loop(spans[0], spans[1], body)
+
+    def to_filter_start(base, tab, source):
+        run(unit(0, 0), lambda job: analyse(base, tab, 0, job))
         for low, high, part, behind in (
-            (0, lag, 0, None),
-            (lag, per_pass, 0, 0),
-            (per_pass, per_pass + lag, 1, 0),
-            (per_pass + lag, jobs, 1, 1),
+            (pairs, per_pass, 0, 0),
+            (per_pass, per_pass + pairs, 1, 0),
+            (per_pass + pairs, per_pass + 2 * pairs, 1, 1),
         ):
 
             def step(job):
+                settle(base, source, behind, job - pairs)
                 analyse(base, tab, part, job)
-                if behind is not None:
-                    settle(base, source, behind, job - lag)
 
             loop(low, high, step)
+        loop(per_pass + 2 * pairs, jobs, lambda job: analyse(base, tab, 1, job))
+
+    def through_filter(base, tab, source, make):
         filter_part(base, 0, source, make)
-        settle(base, source, 1, jobs - lag)
-        loop(0, per_pass, lambda job: relay(base, 0, job))
-        for job in range(jobs - lag + 1, jobs):
-            settle(base, source, 1, job)
+        run(unit(1, 1), lambda job: settle(base, source, 1, job))
+        run(unit(0, 0), lambda job: relay(base, 0, job))
+        run(unit(1, 2), lambda job: settle(base, source, 1, job))
+        run(unit(0, 1), lambda job: relay(base, 0, job))
         filter_part(base, 1, source, make)
-
-    def from_filter(base, tab, finish):
-        def step(job):
-            synthesise(base, tab, 0, job)
-            relay(base, 1, job + per_pass)
-
-        loop(0, per_pass, step)
-        for chunk in range(chunks):
-            first = per_pass + chunk * pairs
-            loop(first, first + pairs, lambda job: synthesise(base, tab, 1, job))
-            if chunk:
-                finish(chunk - 1)
-        finish(chunks - 1)
+        run(unit(0, 0), lambda job: synthesise(base, tab, 0, job))
+        run(unit(1, 0), lambda job: relay(base, 1, job))
+        run(unit(0, 2), lambda job: relay(base, 0, job))
+        loop(per_pass + pairs, jobs, lambda job: relay(base, 1, job))
 
     def spread(stage, chunk, part):
         for kind in range(part * pairs, (part + 1) * pairs):
             to_owners(stage, kind, chunk, band_out, lat_spot, lat_dev)
 
-    for chunk in range(chunks):
-        load(chunk).wait()
-
-        def fourier(row, carry):
-            put_pair(band_out, chunk, row, dot(fwd_fk[...], pair(fbuf, chunk, row)))
-            return carry
-
-        lax.fori_loop(0, lat_dev // 2, fourier, 0)
-        spread(0, chunk, 0)
-    for chunk in range(chunks):
-        spread(0, chunk, 1)
     fill_tables(
         side, [group(kind, column) * orders for kind in range(kinds)], deg_ref, diag_ref, cos_ref,
         quad_ref, qtab, ptab, table, wide_b,
     )
+    for chunk in range(chunks):
+        load(chunk).wait()
+
+        def fourier(row, carry):
+            put_pair(band_out, chunk, row, dot(fwd_fk[...], pair(fbuf, chunk, row)))
+            return carry
+
+        lax.fori_loop(0, lat_dev // 2, fourier, 0)
+        if chunk == 0:
+            pl.semaphore_wait(barrier, n - 1 + nb - 1)
+        spread(0, chunk, 0)
+    for chunk in range(chunks):
+        spread(0, chunk, 1)
     spots = lax.broadcasted_iota(jnp.int32, row_ref.shape, 1)
 
     def invert(slot, carry):
@@ -781,7 +783,8 @@
     turn.start()
     turn.wait()
     load_w.wait()
-    to_filter(0, qtab, co, mix)
+    to_filter_start(0, qtab, co)
+    through_filter(0, ptab, co, mix)
 
     def between(chunk):
         load_cot(chunk).wait()
@@ -797,11 +800,38 @@
 
         lax.fori_loop(0, lat_dev // 2, middle, 0)
         spread(6, chunk, 0)
-
-    from_filter(0, ptab, between)
-    for chunk in range(chunks):
         spread(6, chunk, 1)
-    to_filter(6, ptab, go, adjoint)
+
+    def forth(part, low, high):
+        loop(low, high, lambda job: analyse(6, ptab, part, job))
+
+    def back(part, low, high):
+        loop(low, high, lambda job: settle(6, go, part, job))
+
+    def synth(base, tab, part, low, high):
+        loop(low, high, lambda job: synthesise(base, tab, part, job))
+
+    far = per_pass
+    synth(0, ptab, 0, 2, 4)
+    synth(0, ptab, 1, far, far + 2)
+    synth(0, ptab, 0, 4, 5)
+    between(0)
+    synth(0, ptab, 0, 5, 6)
+    forth(0, 0, 2)
+    synth(0, ptab, 1, far + 2, far + 4)
+    forth(1, far, far + 2)
+    synth(0, ptab, 1, far + 4, far + 6)
+    between(1)
+    back(0, 0, 1)
+    between(2)
+    back(0, 1, 2)
+    forth(0, 2, 4)
+    back(1, far, far + 2)
+    forth(0, 4, 6)
+    back(0, 2, 4)
+    forth(1, far + 2, far + 6)
+    back(0, 4, 6)
+    through_filter(6, qtab, go, adjoint)
 
     def weight_grad(slot, carry):
         values = joined(co, slot, slice(None))
@@ -858,7 +888,15 @@
         lax.fori_loop(0, lat_dev // 2, finish, 0)
         store(chunk).start()
 
-    from_filter(6, qtab, last)
+    synth(6, qtab, 0, 2, 4)
+    synth(6, qtab, 1, far, far + 2)
+    synth(6, qtab, 0, 4, 5)
+    last(0)
+    synth(6, qtab, 0, 5, 6)
+    synth(6, qtab, 1, far + 2, far + 4)
+    synth(6, qtab, 1, far + 4, far + 6)
+    last(1)
+    last(2)
     for chunk in range(chunks):
         for kind in range(kinds):
             left_for_owners(6, kind, chunk, band_out)
@@ -932,7 +970,8 @@
             buffer(chunks, slots, n * rows, LANES),
             buffer(chunks, slots, n * rows, LANES),
             pltpu.VMEM((wide_rows, LANES), jnp.float32),
-            pltpu.VMEM((3 * wide_rows, LANES), jnp.float32),
+            pltpu.VMEM((4 * wide_rows, LANES), jnp.float32),
+            pltpu.VMEM((side_lats * rows, LANES), jnp.float32),
             buffer(*weights.shape),
             buffer(others, *weights.shape),
             buffer(kinds, GROUP, DEGREES, side_lats),

time: 290 us -> 278 us (0.959)
  Pallas kernels: 283 us -> 271 us
    pallas_call x1, Pallas kernels: 283 us -> 271 us  [local_kernel(): pl.pallas_call(functools.partial(block_kernel, n, nb), out_shape=(jax.Sha...]
where the time goes in v3:
time: 278 us
  Pallas kernels  271 us (97%)
  local copies, waits for them, and re-layouts  6.5 us (2%)
    pallas_call x1, Pallas kernels, local_kernel(): pl.pallas_call(functools.partial(block_kernel, n, nb), out_shape=(jax.Sha...  271 us
    unnamed x4, local copies, waits for them, and re-layouts  6.5 us

profile of v3, /device:TPU:0, one launch (start us, length us, event | category | flops | bytes accessed | tf_op | source)
XLA Modules:
  0.0 277.8 jit_solution(924171210121379598)
XLA Ops:
  0.6 270.6 %filter_block.1 = (bf16[1,12,384,384]{3,2,1,0:T(8,128)(2,1)}, bf16[8,2,384,384]{3,2,1,0:T(8,128)(2,1)}) custom-call(bf16[1,12,384,384]{3,2,1,0:T(8,128)(2,1)} %fields.1, bf16[1,12,384,384]{3,2,1,0:T(8,128)(2,1)} %cotangent.1, bf16[8,2,384,384]{3,2,1,0:T(8,128)(2,1)} %weights.1, s32[128]{0:T(128)} %deg_ref.1, f32[2,128,128]{2,1,0:T(8,128)} %constant.14.clone.diag_ref, ...), custom_call_target="tpu_custom_call" | custom-call | tf_op jit(solution)/shard_map/filter_block/pallas_call | solution.py:948
  271.3 0.0 copy-start
  271.3 4.3 %copy.15 = bf16[1,12,384,384]{3,2,1,0:T(8,128)(2,1)} copy(bf16[1,12,384,384]{3,2,1,0:T(8,128)(2,1)} %get-tuple-element.4) | data formatting | bytes 7077888
  275.6 0.0 copy-done
  275.6 2.2 copy.16
Async XLA Ops:
  271.3 4.3 %copy-start = (bf16[8,2,384,384]{3,2,1,0:T(8,128)(2,1)S(1)}, bf16[8,2,384,384]{3,2,1,0:T(8,128)(2,1)}, u32[]{:S(2)}) copy-start(bf16[8,2,384,384]{3,2,1,0:T(8,128)(2,1)} %get-tuple-element.5) | copy-start | bytes 14155780

commit v4 on v3

--- a/solution.py
+++ b/solution.py
@@ -237,7 +237,7 @@
         return tuple(state)
 
     zeros = cosine * 0.0
-    lax.fori_loop(0, degrees, advance, ((zeros, zeros),) * kinds)
+    lax.fori_loop(0, degrees, advance, ((zeros, zeros),) * kinds, unroll=2)
 
     ahead = every // 2
     tail = degrees // 2
@@ -485,7 +485,7 @@
             result_ref[pl.ds(start + 2 * order + 1, depth_out, stride=rows), :] = result[:, LANES:]
             return carry
 
-        lax.fori_loop(0, orders, one, 0)
+        lax.fori_loop(0, orders, one, 0, unroll=8)
 
     def narrow(source, target, place, chunk, start, depth, count):
         def one(block, carry):
@@ -713,7 +713,7 @@
             if base:
                 for kind in part_kinds:
                     left_for_owners(3, kind, chunk, mixed)
-            lax.fori_loop(0, slots, make(part, chunk), 0)
+            lax.fori_loop(0, slots, make(part, chunk), 0, unroll=4)
             for kind in part_kinds:
                 to_owners(base + 3, kind, chunk, mixed, slot_spot, slots)
 
@@ -746,8 +746,8 @@
         run(unit(0, 0), lambda job: relay(base, 0, job))
         run(unit(1, 2), lambda job: settle(base, source, 1, job))
         run(unit(0, 1), lambda job: relay(base, 0, job))
+        run(unit(0, 0), lambda job: synthesise(base, tab, 0, job))
         filter_part(base, 1, source, make)
-        run(unit(0, 0), lambda job: synthesise(base, tab, 0, job))
         run(unit(1, 0), lambda job: relay(base, 1, job))
         run(unit(0, 2), lambda job: relay(base, 0, job))
         loop(per_pass + pairs, jobs, lambda job: relay(base, 1, job))
@@ -756,20 +756,26 @@
         for kind in range(part * pairs, (part + 1) * pairs):
             to_owners(stage, kind, chunk, band_out, lat_spot, lat_dev)
 
+    def transform(chunk):
+        load(chunk).wait()
+
+        def fourier(row, carry):
+            put_pair(band_out, chunk, row, dot(fwd_fk[...], pair(fbuf, chunk, row)))
+            return carry
+
+        lax.fori_loop(0, lat_dev // 2, fourier, 0, unroll=3)
+
+    transform(0)
+    pl.semaphore_wait(barrier, n - 1 + nb - 1)
+    spread(0, 0, 0)
+    transform(1)
+    spread(0, 1, 0)
     fill_tables(
         side, [group(kind, column) * orders for kind in range(kinds)], deg_ref, diag_ref, cos_ref,
         quad_ref, qtab, ptab, table, wide_b,
     )
-    for chunk in range(chunks):
-        load(chunk).wait()
-
-        def fourier(row, carry):
-            put_pair(band_out, chunk, row, dot(fwd_fk[...], pair(fbuf, chunk, row)))
-            return carry
-
-        lax.fori_loop(0, lat_dev // 2, fourier, 0)
-        if chunk == 0:
-            pl.semaphore_wait(barrier, n - 1 + nb - 1)
+    for chunk in range(2, chunks):
+        transform(chunk)
         spread(0, chunk, 0)
     for chunk in range(chunks):
         spread(0, chunk, 1)
@@ -798,15 +804,9 @@
             put_pair(band_out, chunk, row, dot(inv_fk[...], upstream.astype(jnp.bfloat16)))
             return carry
 
-        lax.fori_loop(0, lat_dev // 2, middle, 0)
+        lax.fori_loop(0, lat_dev // 2, middle, 0, unroll=3)
         spread(6, chunk, 0)
         spread(6, chunk, 1)
-
-    def forth(part, low, high):
-        loop(low, high, lambda job: analyse(6, ptab, part, job))
-
-    def back(part, low, high):
-        loop(low, high, lambda job: settle(6, go, part, job))
 
     def synth(base, tab, part, low, high):
         loop(low, high, lambda job: synthesise(base, tab, part, job))
@@ -817,20 +817,10 @@
     synth(0, ptab, 0, 4, 5)
     between(0)
     synth(0, ptab, 0, 5, 6)
-    forth(0, 0, 2)
-    synth(0, ptab, 1, far + 2, far + 4)
-    forth(1, far, far + 2)
-    synth(0, ptab, 1, far + 4, far + 6)
+    synth(0, ptab, 1, far + 2, far + 6)
     between(1)
-    back(0, 0, 1)
     between(2)
-    back(0, 1, 2)
-    forth(0, 2, 4)
-    back(1, far, far + 2)
-    forth(0, 4, 6)
-    back(0, 2, 4)
-    forth(1, far + 2, far + 6)
-    back(0, 4, 6)
+    to_filter_start(6, ptab, go)
     through_filter(6, qtab, go, adjoint)
 
     def weight_grad(slot, carry):
@@ -885,7 +875,7 @@
             put_pair(cbuf, chunk, row, pair(cbuf, chunk, row).astype(jnp.float32) + delta)
             return carry
 
-        lax.fori_loop(0, lat_dev // 2, finish, 0)
+        lax.fori_loop(0, lat_dev // 2, finish, 0, unroll=3)
         store(chunk).start()
 
     synth(6, qtab, 0, 2, 4)
@@ -893,8 +883,7 @@
     synth(6, qtab, 0, 4, 5)
     last(0)
     synth(6, qtab, 0, 5, 6)
-    synth(6, qtab, 1, far + 2, far + 4)
-    synth(6, qtab, 1, far + 4, far + 6)
+    synth(6, qtab, 1, far + 2, far + 6)
     last(1)
     last(2)
     for chunk in range(chunks):

time: 278 us -> 273 us (0.982)
  Pallas kernels: 271 us -> 264 us
    pallas_call x1, Pallas kernels: 271 us -> 264 us  [local_kernel(): pl.pallas_call(functools.partial(block_kernel, n, nb), out_shape=(jax.Sha...]
where the time goes in v4:
time: 273 us; the launch traced here: 271 us
  Pallas kernels  264 us (97%)
  local copies, waits for them, and re-layouts  6.5 us (2%)
    pallas_call x1, Pallas kernels, local_kernel(): pl.pallas_call(functools.partial(block_kernel, n, nb), out_shape=(jax.Sha...  264 us
    unnamed x4, local copies, waits for them, and re-layouts  6.5 us

profile of v4, /device:TPU:0, one launch (start us, length us, event | category | flops | bytes accessed | tf_op | source)
XLA Modules:
  0.0 271.1 jit_solution(17572651289710575791)
XLA Ops:
  0.6 264.0 %filter_block.1 = (bf16[1,12,384,384]{3,2,1,0:T(8,128)(2,1)}, bf16[8,2,384,384]{3,2,1,0:T(8,128)(2,1)}) custom-call(bf16[1,12,384,384]{3,2,1,0:T(8,128)(2,1)} %fields.1, bf16[1,12,384,384]{3,2,1,0:T(8,128)(2,1)} %cotangent.1, bf16[8,2,384,384]{3,2,1,0:T(8,128)(2,1)} %weights.1, s32[128]{0:T(128)} %deg_ref.1, f32[2,128,128]{2,1,0:T(8,128)} %constant.14.clone.diag_ref, ...), custom_call_target="tpu_custom_call" | custom-call | tf_op jit(solution)/shard_map/filter_block/pallas_call | solution.py:937
  264.6 0.0 copy-start
  264.6 4.3 %copy.15 = bf16[1,12,384,384]{3,2,1,0:T(8,128)(2,1)} copy(bf16[1,12,384,384]{3,2,1,0:T(8,128)(2,1)} %get-tuple-element.4) | data formatting | bytes 7077888
  268.9 0.0 copy-done
  268.9 2.2 copy.16
Async XLA Ops:
  264.6 4.3 %copy-start = (bf16[8,2,384,384]{3,2,1,0:T(8,128)(2,1)S(1)}, bf16[8,2,384,384]{3,2,1,0:T(8,128)(2,1)}, u32[]{:S(2)}) copy-start(bf16[8,2,384,384]{3,2,1,0:T(8,128)(2,1)} %get-tuple-element.5) | copy-start | bytes 14155780

commit v5 on v4

--- a/solution.py
+++ b/solution.py
@@ -485,7 +485,7 @@
             result_ref[pl.ds(start + 2 * order + 1, depth_out, stride=rows), :] = result[:, LANES:]
             return carry
 
-        lax.fori_loop(0, orders, one, 0, unroll=8)
+        lax.fori_loop(0, orders, one, 0, unroll=4)
 
     def narrow(source, target, place, chunk, start, depth, count):
         def one(block, carry):
@@ -725,8 +725,10 @@
     def run(spans, body):
         loop(spans[0], spans[1], body)
 
-    def to_filter_start(base, tab, source):
-        run(unit(0, 0), lambda job: analyse(base, tab, 0, job))
+    def to_filter_start(base, tab, source, between_first):
+        loop(0, 1, lambda job: analyse(base, tab, 0, job))
+        between_first()
+        loop(1, pairs, lambda job: analyse(base, tab, 0, job))
         for low, high, part, behind in (
             (pairs, per_pass, 0, 0),
             (per_pass, per_pass + pairs, 1, 0),
@@ -747,10 +749,11 @@
         run(unit(1, 2), lambda job: settle(base, source, 1, job))
         run(unit(0, 1), lambda job: relay(base, 0, job))
         run(unit(0, 0), lambda job: synthesise(base, tab, 0, job))
+        run(unit(0, 2), lambda job: relay(base, 0, job))
+        loop(pairs, pairs + 1, lambda job: synthesise(base, tab, 0, job))
         filter_part(base, 1, source, make)
-        run(unit(1, 0), lambda job: relay(base, 1, job))
-        run(unit(0, 2), lambda job: relay(base, 0, job))
-        loop(per_pass + pairs, jobs, lambda job: relay(base, 1, job))
+        loop(pairs + 1, 2 * pairs, lambda job: synthesise(base, tab, 0, job))
+        loop(per_pass, jobs, lambda job: relay(base, 1, job))
 
     def spread(stage, chunk, part):
         for kind in range(part * pairs, (part + 1) * pairs):
@@ -789,7 +792,7 @@
     turn.start()
     turn.wait()
     load_w.wait()
-    to_filter_start(0, qtab, co)
+    to_filter_start(0, qtab, co, lambda: None)
     through_filter(0, ptab, co, mix)
 
     def between(chunk):
@@ -808,19 +811,21 @@
         spread(6, chunk, 0)
         spread(6, chunk, 1)
 
-    def synth(base, tab, part, low, high):
-        loop(low, high, lambda job: synthesise(base, tab, part, job))
-
-    far = per_pass
-    synth(0, ptab, 0, 2, 4)
-    synth(0, ptab, 1, far, far + 2)
-    synth(0, ptab, 0, 4, 5)
-    between(0)
-    synth(0, ptab, 0, 5, 6)
-    synth(0, ptab, 1, far + 2, far + 6)
-    between(1)
-    between(2)
-    to_filter_start(6, ptab, go)
+    def finish_synthesis(base, tab, finish):
+        def apart(chunk):
+            loop(0, 1, lambda step: synthesise(base, tab, 1, per_pass + chunk * pairs + step))
+
+        loop(
+            0, chunks, lambda step: synthesise(base, tab, 1, per_pass + (step + 1) * pairs - 1)
+        )
+        loop(2 * pairs, per_pass, lambda job: synthesise(base, tab, 0, job))
+        apart(0)
+        for chunk in range(1, chunks):
+            apart(chunk)
+            finish(chunk - 1)
+
+    finish_synthesis(0, ptab, between)
+    to_filter_start(6, ptab, go, lambda: between(chunks - 1))
     through_filter(6, qtab, go, adjoint)
 
     def weight_grad(slot, carry):
@@ -878,14 +883,8 @@
         lax.fori_loop(0, lat_dev // 2, finish, 0, unroll=3)
         store(chunk).start()
 
-    synth(6, qtab, 0, 2, 4)
-    synth(6, qtab, 1, far, far + 2)
-    synth(6, qtab, 0, 4, 5)
-    last(0)
-    synth(6, qtab, 0, 5, 6)
-    synth(6, qtab, 1, far + 2, far + 6)
-    last(1)
-    last(2)
+    finish_synthesis(6, qtab, last)
+    last(chunks - 1)
     for chunk in range(chunks):
         for kind in range(kinds):
             left_for_owners(6, kind, chunk, band_out)

time: 273 us -> 267 us (0.978)
  Pallas kernels: 264 us -> 259 us
    pallas_call x1, Pallas kernels: 264 us -> 259 us  [local_kernel(): pl.pallas_call(functools.partial(block_kernel, n, nb), out_shape=(jax.Sha...]
where the time goes in v5:
time: 267 us; the launch traced here: 266 us
  Pallas kernels  259 us (97%)
  local copies, waits for them, and re-layouts  6.5 us (2%)
    pallas_call x1, Pallas kernels, local_kernel(): pl.pallas_call(functools.partial(block_kernel, n, nb), out_shape=(jax.Sha...  259 us
    unnamed x4, local copies, waits for them, and re-layouts  6.5 us

profile of v5, /device:TPU:0, one launch (start us, length us, event | category | flops | bytes accessed | tf_op | source)
XLA Modules:
  0.0 266.0 jit_solution(11289785952628800354)
XLA Ops:
  0.6 258.9 %filter_block.1 = (bf16[1,12,384,384]{3,2,1,0:T(8,128)(2,1)}, bf16[8,2,384,384]{3,2,1,0:T(8,128)(2,1)}) custom-call(bf16[1,12,384,384]{3,2,1,0:T(8,128)(2,1)} %fields.1, bf16[1,12,384,384]{3,2,1,0:T(8,128)(2,1)} %cotangent.1, bf16[8,2,384,384]{3,2,1,0:T(8,128)(2,1)} %weights.1, s32[128]{0:T(128)} %deg_ref.1, f32[2,128,128]{2,1,0:T(8,128)} %constant.14.clone.diag_ref, ...), custom_call_target="tpu_custom_call" | custom-call | tf_op jit(solution)/shard_map/filter_block/pallas_call | solution.py:936
  259.5 0.0 copy-start
  259.5 4.3 %copy.15 = bf16[1,12,384,384]{3,2,1,0:T(8,128)(2,1)} copy(bf16[1,12,384,384]{3,2,1,0:T(8,128)(2,1)} %get-tuple-element.4) | data formatting | bytes 7077888
  263.9 0.0 copy-done
  263.9 2.2 copy.16
Async XLA Ops:
  259.5 4.3 %copy-start = (bf16[8,2,384,384]{3,2,1,0:T(8,128)(2,1)S(1)}, bf16[8,2,384,384]{3,2,1,0:T(8,128)(2,1)}, u32[]{:S(2)}) copy-start(bf16[8,2,384,384]{3,2,1,0:T(8,128)(2,1)} %get-tuple-element.5) | copy-start | bytes 14155780

commit v6 on v5

--- a/solution.py
+++ b/solution.py
@@ -726,9 +726,8 @@
         loop(spans[0], spans[1], body)
 
     def to_filter_start(base, tab, source, between_first):
-        loop(0, 1, lambda job: analyse(base, tab, 0, job))
+        run(unit(0, 0), lambda job: analyse(base, tab, 0, job))
         between_first()
-        loop(1, pairs, lambda job: analyse(base, tab, 0, job))
         for low, high, part, behind in (
             (pairs, per_pass, 0, 0),
             (per_pass, per_pass + pairs, 1, 0),
@@ -749,11 +748,12 @@
         run(unit(1, 2), lambda job: settle(base, source, 1, job))
         run(unit(0, 1), lambda job: relay(base, 0, job))
         run(unit(0, 0), lambda job: synthesise(base, tab, 0, job))
-        run(unit(0, 2), lambda job: relay(base, 0, job))
         loop(pairs, pairs + 1, lambda job: synthesise(base, tab, 0, job))
         filter_part(base, 1, source, make)
         loop(pairs + 1, 2 * pairs, lambda job: synthesise(base, tab, 0, job))
-        loop(per_pass, jobs, lambda job: relay(base, 1, job))
+        run(unit(1, 0), lambda job: relay(base, 1, job))
+        run(unit(0, 2), lambda job: relay(base, 0, job))
+        run(unit(1, 1), lambda job: relay(base, 1, job))
 
     def spread(stage, chunk, part):
         for kind in range(part * pairs, (part + 1) * pairs):
@@ -812,20 +812,20 @@
         spread(6, chunk, 1)
 
     def finish_synthesis(base, tab, finish):
-        def apart(chunk):
-            loop(0, 1, lambda step: synthesise(base, tab, 1, per_pass + chunk * pairs + step))
-
-        loop(
-            0, chunks, lambda step: synthesise(base, tab, 1, per_pass + (step + 1) * pairs - 1)
-        )
-        loop(2 * pairs, per_pass, lambda job: synthesise(base, tab, 0, job))
-        apart(0)
+        first, second = unit(0, 2)
+        run(unit(1, 0), lambda job: synthesise(base, tab, 1, job))
+        loop(first, first + 1, lambda job: synthesise(base, tab, 0, job))
+        run(unit(1, 2), lambda job: relay(base, 1, job))
+        finish(0)
+        loop(first + 1, second, lambda job: synthesise(base, tab, 0, job))
+        loop(per_pass + pairs, jobs, lambda job: synthesise(base, tab, 1, job))
+
+    def rest(finish):
         for chunk in range(1, chunks):
-            apart(chunk)
-            finish(chunk - 1)
+            finish(chunk)
 
     finish_synthesis(0, ptab, between)
-    to_filter_start(6, ptab, go, lambda: between(chunks - 1))
+    to_filter_start(6, ptab, go, lambda: rest(between))
     through_filter(6, qtab, go, adjoint)
 
     def weight_grad(slot, carry):
@@ -884,7 +884,7 @@
         store(chunk).start()
 
     finish_synthesis(6, qtab, last)
-    last(chunks - 1)
+    rest(last)
     for chunk in range(chunks):
         for kind in range(kinds):
             left_for_owners(6, kind, chunk, band_out)

time: 267 us -> 269 us (level)
  Pallas kernels: 259 us -> 262 us
where the time goes in v6:
time: 269 us
  Pallas kernels  262 us (97%)
  local copies, waits for them, and re-layouts  6.5 us (2%)
    pallas_call x1, Pallas kernels, local_kernel(): pl.pallas_call(functools.partial(block_kernel, n, nb), out_shape=(jax.Sha...  262 us
    unnamed x4, local copies, waits for them, and re-layouts  6.5 us

profile of v6, /device:TPU:0, one launch (start us, length us, event | category | flops | bytes accessed | tf_op | source)
XLA Modules:
  0.0 268.7 jit_solution(16977787789457716005)
XLA Ops:
  0.6 261.6 %filter_block.1 = (bf16[1,12,384,384]{3,2,1,0:T(8,128)(2,1)}, bf16[8,2,384,384]{3,2,1,0:T(8,128)(2,1)}) custom-call(bf16[1,12,384,384]{3,2,1,0:T(8,128)(2,1)} %fields.1, bf16[1,12,384,384]{3,2,1,0:T(8,128)(2,1)} %cotangent.1, bf16[8,2,384,384]{3,2,1,0:T(8,128)(2,1)} %weights.1, s32[128]{0:T(128)} %deg_ref.1, f32[2,128,128]{2,1,0:T(8,128)} %constant.14.clone.diag_ref, ...), custom_call_target="tpu_custom_call" | custom-call | tf_op jit(solution)/shard_map/filter_block/pallas_call | solution.py:936
  262.2 0.0 copy-start
  262.2 4.3 %copy.15 = bf16[1,12,384,384]{3,2,1,0:T(8,128)(2,1)} copy(bf16[1,12,384,384]{3,2,1,0:T(8,128)(2,1)} %get-tuple-element.4) | data formatting | bytes 7077888
  266.5 0.0 copy-done
  266.5 2.2 copy.16
Async XLA Ops:
  262.2 4.3 %copy-start = (bf16[8,2,384,384]{3,2,1,0:T(8,128)(2,1)S(1)}, bf16[8,2,384,384]{3,2,1,0:T(8,128)(2,1)}, u32[]{:S(2)}) copy-start(bf16[8,2,384,384]{3,2,1,0:T(8,128)(2,1)} %get-tuple-element.5) | copy-start | bytes 14155780

commit v7 on v6

--- a/solution.py
+++ b/solution.py
@@ -725,9 +725,8 @@
     def run(spans, body):
         loop(spans[0], spans[1], body)
 
-    def to_filter_start(base, tab, source, between_first):
+    def to_filter_start(base, tab, source):
         run(unit(0, 0), lambda job: analyse(base, tab, 0, job))
-        between_first()
         for low, high, part, behind in (
             (pairs, per_pass, 0, 0),
             (per_pass, per_pass + pairs, 1, 0),
@@ -740,6 +739,24 @@
 
             loop(low, high, step)
         loop(per_pass + 2 * pairs, jobs, lambda job: analyse(base, tab, 1, job))
+
+    def to_filter_by_chunk(base, tab, source, rest):
+        run(unit(0, 0), lambda job: analyse(base, tab, 0, job))
+        run(unit(1, 0), lambda job: analyse(base, tab, 1, job))
+        rest()
+
+        def second(job):
+            settle(base, source, 0, job - pairs)
+            analyse(base, tab, 0, job)
+
+        run(unit(0, 1), second)
+        run(unit(1, 0), lambda job: settle(base, source, 1, job))
+        run(unit(0, 2), lambda job: analyse(base, tab, 0, job))
+
+        for job in range(pairs, 2 * pairs):
+            settle(base, source, 0, job)
+            run(unit(1, job - pairs + 1), lambda spot: analyse(base, tab, 1, spot))
+        run(unit(0, 2), lambda job: settle(base, source, 0, job))
 
     def through_filter(base, tab, source, make):
         filter_part(base, 0, source, make)
@@ -792,7 +809,7 @@
     turn.start()
     turn.wait()
     load_w.wait()
-    to_filter_start(0, qtab, co, lambda: None)
+    to_filter_start(0, qtab, co)
     through_filter(0, ptab, co, mix)
 
     def between(chunk):
@@ -816,16 +833,19 @@
         run(unit(1, 0), lambda job: synthesise(base, tab, 1, job))
         loop(first, first + 1, lambda job: synthesise(base, tab, 0, job))
         run(unit(1, 2), lambda job: relay(base, 1, job))
-        finish(0)
+        if not base:
+            finish(0)
         loop(first + 1, second, lambda job: synthesise(base, tab, 0, job))
         loop(per_pass + pairs, jobs, lambda job: synthesise(base, tab, 1, job))
+        if base:
+            finish(0)
 
     def rest(finish):
         for chunk in range(1, chunks):
             finish(chunk)
 
     finish_synthesis(0, ptab, between)
-    to_filter_start(6, ptab, go, lambda: rest(between))
+    to_filter_by_chunk(6, ptab, go, lambda: rest(between))
     through_filter(6, qtab, go, adjoint)
 
     def weight_grad(slot, carry):

time: 269 us -> 261 us (0.970)
  Pallas kernels: 262 us -> 254 us
    pallas_call x1, Pallas kernels: 262 us -> 254 us  [local_kernel(): pl.pallas_call(functools.partial(block_kernel, n, nb), out_shape=(jax.Sha...]
where the time goes in v7:
time: 261 us
  Pallas kernels  254 us (97%)
  local copies, waits for them, and re-layouts  6.5 us (2%)
    pallas_call x1, Pallas kernels, local_kernel(): pl.pallas_call(functools.partial(block_kernel, n, nb), out_shape=(jax.Sha...  254 us
    unnamed x4, local copies, waits for them, and re-layouts  6.5 us

profile of v7, /device:TPU:0, one launch (start us, length us, event | category | flops | bytes accessed | tf_op | source)
XLA Modules:
  0.0 260.8 jit_solution(5629425255282999031)
XLA Ops:
  0.6 253.6 %filter_block.1 = (bf16[1,12,384,384]{3,2,1,0:T(8,128)(2,1)}, bf16[8,2,384,384]{3,2,1,0:T(8,128)(2,1)}) custom-call(bf16[1,12,384,384]{3,2,1,0:T(8,128)(2,1)} %fields.1, bf16[1,12,384,384]{3,2,1,0:T(8,128)(2,1)} %cotangent.1, bf16[8,2,384,384]{3,2,1,0:T(8,128)(2,1)} %weights.1, s32[128]{0:T(128)} %deg_ref.1, f32[2,128,128]{2,1,0:T(8,128)} %constant.14.clone.diag_ref, ...), custom_call_target="tpu_custom_call" | custom-call | tf_op jit(solution)/shard_map/filter_block/pallas_call | solution.py:956
  254.3 0.0 copy-start
  254.3 4.3 %copy.15 = bf16[1,12,384,384]{3,2,1,0:T(8,128)(2,1)} copy(bf16[1,12,384,384]{3,2,1,0:T(8,128)(2,1)} %get-tuple-element.4) | data formatting | bytes 7077888
  258.6 0.0 copy-done
  258.6 2.2 copy.16
Async XLA Ops:
  254.3 4.3 %copy-start = (bf16[8,2,384,384]{3,2,1,0:T(8,128)(2,1)S(1)}, bf16[8,2,384,384]{3,2,1,0:T(8,128)(2,1)}, u32[]{:S(2)}) copy-start(bf16[8,2,384,384]{3,2,1,0:T(8,128)(2,1)} %get-tuple-element.5) | copy-start | bytes 14155780

commit v8 on v7

--- a/solution.py
+++ b/solution.py
@@ -826,7 +826,11 @@
 
         lax.fori_loop(0, lat_dev // 2, middle, 0, unroll=3)
         spread(6, chunk, 0)
-        spread(6, chunk, 1)
+        if chunk == 0:
+            spread(6, 0, 1)
+        if chunk == chunks - 1:
+            for earlier in range(1, chunks):
+                spread(6, earlier, 1)
 
     def finish_synthesis(base, tab, finish):
         first, second = unit(0, 2)

time: 261 us -> 260 us (level)
  no operation moved by 1% of the time
where the time goes in v8:
time: 260 us; the launch traced here: 259 us
  Pallas kernels  252 us (97%)
  local copies, waits for them, and re-layouts  6.5 us (2%)
    pallas_call x1, Pallas kernels, local_kernel(): pl.pallas_call(functools.partial(block_kernel, n, nb), out_shape=(jax.Sha...  252 us
    unnamed x4, local copies, waits for them, and re-layouts  6.5 us

profile of v8, /device:TPU:0, one launch (start us, length us, event | category | flops | bytes accessed | tf_op | source)
XLA Modules:
  0.0 259.5 jit_solution(8524050897157621551)
XLA Ops:
  0.6 252.3 %filter_block.1 = (bf16[1,12,384,384]{3,2,1,0:T(8,128)(2,1)}, bf16[8,2,384,384]{3,2,1,0:T(8,128)(2,1)}) custom-call(bf16[1,12,384,384]{3,2,1,0:T(8,128)(2,1)} %fields.1, bf16[1,12,384,384]{3,2,1,0:T(8,128)(2,1)} %cotangent.1, bf16[8,2,384,384]{3,2,1,0:T(8,128)(2,1)} %weights.1, s32[128]{0:T(128)} %deg_ref.1, f32[2,128,128]{2,1,0:T(8,128)} %constant.14.clone.diag_ref, ...), custom_call_target="tpu_custom_call" | custom-call | tf_op jit(solution)/shard_map/filter_block/pallas_call | solution.py:960
  253.0 0.0 copy-start
  253.0 4.3 %copy.15 = bf16[1,12,384,384]{3,2,1,0:T(8,128)(2,1)} copy(bf16[1,12,384,384]{3,2,1,0:T(8,128)(2,1)} %get-tuple-element.4) | data formatting | bytes 7077888
  257.3 0.0 copy-done
  257.3 2.2 copy.16
Async XLA Ops:
  253.0 4.3 %copy-start = (bf16[8,2,384,384]{3,2,1,0:T(8,128)(2,1)S(1)}, bf16[8,2,384,384]{3,2,1,0:T(8,128)(2,1)}, u32[]{:S(2)}) copy-start(bf16[8,2,384,384]{3,2,1,0:T(8,128)(2,1)} %get-tuple-element.5) | copy-start | bytes 14155780

commit v9 on v8

--- a/solution.py
+++ b/solution.py
@@ -290,10 +290,10 @@
 def block_kernel(
     n, nb, fields, cotangent, weights, deg_ref, diag_ref, cos_ref, quad_ref,
     fwd_fk, fwd_kf, inv_fk, inv_kf,
-    grad_out, dw_out,
-    fbuf, cbuf, wbuf, band_out, band_in, ord_in, ord_out, cross_out, cross_in, slot_out, slot_all,
-    tail_out, co, go, mixed, wide_a, wide_b, wide_c, dw, dw_in, qtab, ptab, table, row_ref, slot_of, by_name,
-    load_sem, send_sem, recv_sem, dw_send, dw_recv, out_sem,
+    grad_out, dw,
+    fbuf, wbuf, band_out, band_in, ord_in, ord_out, cross_out, cross_in, slot_out, slot_all,
+    tail_out, co, go, mixed, wide_a, wide_b, wide_c, dw_in, qtab, ptab, table, row_ref, slot_of, by_name,
+    load_sem, send_sem, recv_sem, dw_send, dw_recv,
 ):
     me = lax.axis_index("lat")
     me_b = lax.axis_index("batch")
@@ -366,7 +366,9 @@
 
     def load_cot(chunk):
         return pltpu.make_async_copy(
-            cotangent.at[0, :, :, lanes(chunk)], cbuf.at[chunk], load_sem.at[chunks + chunk]
+            cotangent.at[0, :, :, lanes(chunk)],
+            grad_out.at[0, :, :, lanes(chunk)],
+            load_sem.at[chunks + chunk],
         )
 
     load_w = pltpu.make_async_copy(weights, wbuf, load_sem.at[2 * chunks])
@@ -663,6 +665,18 @@
     def pair(source, chunk, row):
         return jnp.concatenate([source[chunk, 2 * row], source[chunk, 2 * row + 1]], axis=1)
 
+    def field_pair(chunk, row):
+        span = slice(chunk * LANES, (chunk + 1) * LANES)
+        return jnp.concatenate(
+            [grad_out[0, 2 * row, :, span], grad_out[0, 2 * row + 1, :, span]], axis=1
+        )
+
+    def put_field_pair(chunk, row, values):
+        span = slice(chunk * LANES, (chunk + 1) * LANES)
+        values = values.astype(jnp.bfloat16)
+        grad_out[0, 2 * row, :, span] = values[:, :LANES]
+        grad_out[0, 2 * row + 1, :, span] = values[:, LANES:]
+
     def put_pair(target, chunk, row, values):
         values = values.astype(jnp.bfloat16)
         target[chunk, 2 * row] = values[:, :LANES]
@@ -820,7 +834,7 @@
 
         def middle(row, carry):
             response = dot(inv_kf[...], pair(band_in, chunk, row))
-            upstream = pair(cbuf, chunk, row).astype(jnp.float32) * gelu_slope(response)
+            upstream = field_pair(chunk, row).astype(jnp.float32) * gelu_slope(response)
             put_pair(band_out, chunk, row, dot(inv_fk[...], upstream.astype(jnp.bfloat16)))
             return carry
 
@@ -876,13 +890,6 @@
         copy.start()
         dw_copies.append(copy)
 
-    def store(chunk):
-        return pltpu.make_async_copy(
-            cbuf.at[chunk], grad_out.at[0, :, :, lanes(chunk)], out_sem.at[chunk]
-        )
-
-    store_w = pltpu.make_async_copy(dw, dw_out, out_sem.at[chunks])
-
     def total(slot, carry):
         value = dw[slot].astype(jnp.float32)
         for step in range(nb - 1):
@@ -895,17 +902,15 @@
             for copy in dw_copies:
                 copy.wait()
             lax.fori_loop(0, slots, total, 0)
-            store_w.start()
         for kind in range(kinds):
             reached_all(11, kind, chunk, band_in)
 
         def finish(row, carry):
             delta = dot(fwd_kf[...], pair(band_in, chunk, row))
-            put_pair(cbuf, chunk, row, pair(cbuf, chunk, row).astype(jnp.float32) + delta)
+            put_field_pair(chunk, row, field_pair(chunk, row).astype(jnp.float32) + delta)
             return carry
 
         lax.fori_loop(0, lat_dev // 2, finish, 0, unroll=3)
-        store(chunk).start()
 
     finish_synthesis(6, qtab, last)
     rest(last)
@@ -930,9 +935,6 @@
 
     loop(0, per_pass, lambda job: drain(0, job))
     loop(per_pass, jobs, lambda job: drain(1, job))
-    for chunk in range(chunks):
-        store(chunk).wait()
-    store_w.wait()
 
 
 def local_kernel(fields, cotangent, weights, degree_of):
@@ -960,13 +962,12 @@
     return pl.pallas_call(
         functools.partial(block_kernel, n, nb),
         out_shape=(
-            jax.ShapeDtypeStruct(fields.shape, jnp.bfloat16),
-            jax.ShapeDtypeStruct(weights.shape, jnp.bfloat16),
+            pltpu.VMEM(fields.shape, jnp.bfloat16),
+            pltpu.VMEM(weights.shape, jnp.bfloat16),
         ),
         in_specs=[anywhere] * 3 + [pl.BlockSpec(memory_space=pltpu.SMEM)] + [vmem] * 7,
-        out_specs=(anywhere, anywhere),
+        out_specs=(vmem, vmem),
         scratch_shapes=[
-            buffer(chunks, lat_dev, lons, LANES),
             buffer(chunks, lat_dev, lons, LANES),
             buffer(*weights.shape),
             buffer(chunks, lat_dev, n * rows, LANES),
@@ -984,7 +985,6 @@
             pltpu.VMEM((wide_rows, LANES), jnp.float32),
             pltpu.VMEM((4 * wide_rows, LANES), jnp.float32),
             pltpu.VMEM((side_lats * rows, LANES), jnp.float32),
-            buffer(*weights.shape),
             buffer(others, *weights.shape),
             buffer(kinds, GROUP, DEGREES, side_lats),
             buffer(kinds, GROUP, DEGREES, side_lats),
@@ -997,10 +997,9 @@
             dma((12, kinds * chunks)),
             dma((others,)),
             dma((others,)),
-            dma((chunks + 1,)),
         ],
         compiler_params=pltpu.CompilerParams(
-            collective_id=0, has_side_effects=True, vmem_limit_bytes=63 * 2**20
+            collective_id=0, has_side_effects=True, vmem_limit_bytes=54 * 2**20
         ),
         name="filter_block",
     )(

time: 260 us -> 256 us (0.985)
    unnamed x4 -> x2, local copies, waits for them, and re-layouts: 6.5 us -> 3.98 us
where the time goes in v9:
time: 256 us
  Pallas kernels  251 us (98%)
  local copies, waits for them, and re-layouts  3.98 us (2%)
    pallas_call x1, Pallas kernels, local_kernel(): pl.pallas_call(functools.partial(block_kernel, n, nb), out_shape=(pltpu.V...  251 us

profile of v9, /device:TPU:0, one launch (start us, length us, event | category | flops | bytes accessed | tf_op | source)
XLA Modules:
  0.0 255.8 jit_solution(11878142872111297170)
XLA Ops:
  0.6 251.2 %filter_block.1 = (bf16[1,12,384,384]{3,2,1,0:T(8,128)(2,1)S(1)}, bf16[8,2,384,384]{3,2,1,0:T(8,128)(2,1)S(1)}) custom-call(bf16[1,12,384,384]{3,2,1,0:T(8,128)(2,1)} %fields.1, bf16[1,12,384,384]{3,2,1,0:T(8,128)(2,1)} %cotangent.1, bf16[8,2,384,384]{3,2,1,0:T(8,128)(2,1)} %weights.1, s32[128]{0:T(128)} %deg_ref.1, f32[2,128,128]{2,1,0:T(8,128)} %constant.14.clone.diag_ref, ...), custom_call_target="tpu_custom_call" | custom-call | tf_op jit(solution)/shard_map/filter_block/pallas_call | solution.py:962
  251.9 1.8 copy.15
  253.7 2.2 copy.16

commit v10 on v9

--- a/solution.py
+++ b/solution.py
@@ -487,7 +487,7 @@
             result_ref[pl.ds(start + 2 * order + 1, depth_out, stride=rows), :] = result[:, LANES:]
             return carry
 
-        lax.fori_loop(0, orders, one, 0, unroll=4)
+        lax.fori_loop(0, orders, one, 0, unroll=8)
 
     def narrow(source, target, place, chunk, start, depth, count):
         def one(block, carry):

time: 256 us -> 254 us (level)
  no operation moved by 1% of the time
where the time goes in v10:
time: 254 us
  Pallas kernels  249 us (98%)
  local copies, waits for them, and re-layouts  3.98 us (2%)
    pallas_call x1, Pallas kernels, local_kernel(): pl.pallas_call(functools.partial(block_kernel, n, nb), out_shape=(pltpu.V...  249 us

profile of v10, /device:TPU:0, one launch (start us, length us, event | category | flops | bytes accessed | tf_op | source)
XLA Modules:
  0.0 254.1 jit_solution(2290752297682663300)
XLA Ops:
  0.6 249.5 %filter_block.1 = (bf16[1,12,384,384]{3,2,1,0:T(8,128)(2,1)S(1)}, bf16[8,2,384,384]{3,2,1,0:T(8,128)(2,1)S(1)}) custom-call(bf16[1,12,384,384]{3,2,1,0:T(8,128)(2,1)} %fields.1, bf16[1,12,384,384]{3,2,1,0:T(8,128)(2,1)} %cotangent.1, bf16[8,2,384,384]{3,2,1,0:T(8,128)(2,1)} %weights.1, s32[128]{0:T(128)} %deg_ref.1, f32[2,128,128]{2,1,0:T(8,128)} %constant.14.clone.diag_ref, ...), custom_call_target="tpu_custom_call" | custom-call | tf_op jit(solution)/shard_map/filter_block/pallas_call | solution.py:962
  250.1 1.8 copy.15
  251.9 2.2 copy.16

commit v11 on v10

--- a/solution.py
+++ b/solution.py
@@ -372,23 +372,22 @@
         )
 
     load_w = pltpu.make_async_copy(weights, wbuf, load_sem.at[2 * chunks])
+    barrier = pltpu.get_barrier_semaphore()
+
+    def greet(step, carry):
+        peer = lax.rem(me + step, n)
+        pl.semaphore_signal(barrier, inc=1, device_id={"lat": peer}, device_id_type=mesh_id)
+        return carry
+
+    lax.fori_loop(1, n, greet, 0)
+    for step in range(1, nb):
+        peer = lax.rem(me_b + step, nb)
+        pl.semaphore_signal(barrier, inc=1, device_id={"batch": peer}, device_id_type=mesh_id)
     for chunk in range(chunks):
         load(chunk).start()
     load_w.start()
     for chunk in range(chunks):
         load_cot(chunk).start()
-
-    barrier = pltpu.get_barrier_semaphore()
-
-    def greet(step, carry):
-        peer = lax.rem(me + step, n)
-        pl.semaphore_signal(barrier, inc=1, device_id={"lat": peer}, device_id_type=mesh_id)
-        return carry
-
-    lax.fori_loop(1, n, greet, 0)
-    for step in range(1, nb):
-        peer = lax.rem(me_b + step, nb)
-        pl.semaphore_signal(barrier, inc=1, device_id={"batch": peer}, device_id_type=mesh_id)
 
     def remote(stage, job, source, target, peer):
         pltpu.make_async_remote_copy(
@@ -577,7 +576,7 @@
                     slot_out[place, chunk, slot] = by_name[deg_ref[side * own + slot]]
                     return carry
 
-                lax.fori_loop(0, own, pick, 0, unroll=4)
+                lax.fori_loop(0, own, pick, 0, unroll=8)
             else:
 
                 def one(block, carry):

time: 254 us -> 256 us (level)
  no operation moved by 1% of the time
where the time goes in v11:
time: 256 us
  Pallas kernels  251 us (98%)
  local copies, waits for them, and re-layouts  3.98 us (2%)
    pallas_call x1, Pallas kernels, local_kernel(): pl.pallas_call(functools.partial(block_kernel, n, nb), out_shape=(pltpu.V...  251 us

profile of v11, /device:TPU:0, one launch (start us, length us, event | category | flops | bytes accessed | tf_op | source)
XLA Modules:
  0.0 256.0 jit_solution(7860346300149295201)
XLA Ops:
  0.6 251.4 %filter_block.1 = (bf16[1,12,384,384]{3,2,1,0:T(8,128)(2,1)S(1)}, bf16[8,2,384,384]{3,2,1,0:T(8,128)(2,1)S(1)}) custom-call(bf16[1,12,384,384]{3,2,1,0:T(8,128)(2,1)} %fields.1, bf16[1,12,384,384]{3,2,1,0:T(8,128)(2,1)} %cotangent.1, bf16[8,2,384,384]{3,2,1,0:T(8,128)(2,1)} %weights.1, s32[128]{0:T(128)} %deg_ref.1, f32[2,128,128]{2,1,0:T(8,128)} %constant.14.clone.diag_ref, ...), custom_call_target="tpu_custom_call" | custom-call | tf_op jit(solution)/shard_map/filter_block/pallas_call | solution.py:961
  252.0 1.8 copy.15
  253.8 2.2 copy.16
